TPU v7x, 256 devices: a whole 4x4x8 slice. The times are simulated.
256 devices in a mesh: section: 2 (over core), tensor: 2 (over x_lo), dp: 64 (over z, y, x_hi).
Axes of the slice: x: 4 (x_hi: 2, x_lo: 2; x = x_hi * 2 + x_lo), y: 4, z: 8, core: 2. Of those that a mesh axis runs over, the one named last changes fastest.
Arguments:
- exit_hidden: bfloat16 [512, 4, 2048], P('dp', None, ('section', 'tensor')), may hold values from -6 to 6
- exit_depth: int32 [512], P('dp'), may hold values from 0 to 1, as said below
- context_len: int32 [512], P('dp'), may hold values from 48 to 384
- attn_gain: float32 [2, 2048], P('section'), may hold values from 0.1 to 1.9
- w_query: bfloat16 [2, 2048, 2048], P('section', None, 'tensor'), may hold values from -0.125 to 0.125
- w_keyval: bfloat16 [2, 2048, 1024], P('section', None, 'tensor'), may hold values from -0.125 to 0.125
- w_out: bfloat16 [2, 2048, 2048], P('section', 'tensor'), may hold values from -0.125 to 0.125
- kv_cache: bfloat16 [2, 512, 384, 8, 128], P('section', 'dp', None, 'tensor'), may hold values from -400 to 400
- mlp_gain: float32 [2, 2048], P('section'), may hold values from 0.1 to 1.9
- w_gate: bfloat16 [2, 2048, 4096], P('section', 'dp', 'tensor'), may hold values from -0.125 to 0.125
- w_up: bfloat16 [2, 2048, 4096], P('section', 'dp', 'tensor'), may hold values from -0.125 to 0.125
- w_down: bfloat16 [2, 2048, 4096], P('section', 'dp', 'tensor'), may hold values from -0.09375 to 0.09375
Outputs:
- layer_states: bfloat16 [2, 512, 4, 2048], P('section', 'dp', None, 'tensor')
Inputs may be any that keep to these rules, and one draw needn't show every extreme that they name: `exit_depth`: every depth from 0 to 1 is held by some request.
All inputs are finite; a program needn't handle non-finite values.
Results may differ from a plain program's by a relative error of at most 0.019.
Values may be sent and summed in bfloat16 or wider, within the bound.
No kernel may reach another device: no remote copies, remote signals or barrier semaphores. Data moves between devices by JAX's collectives and lax.ppermute only.
A program may use at most 192 MiB of HBM per device.

v0:
```python
import math

import jax
import jax.numpy as jnp
from jax import lax
from jax.sharding import PartitionSpec as P

D = 2048
DRAFT = 4
CTX = 384
R_DEV = 8


EPS = 1e-05
THETA = 500000.0
NEGATIVE = -1e30


def from_everyone(array, axis):
    length = lax.axis_size(axis)
    return lax.all_to_all(
        jnp.broadcast_to(array[None], (length, *array.shape)), axis, 0, 0, tiled=True
    )


def laid_out(blocks, dim):
    shape = list(blocks.shape[1:])
    shape[dim] *= blocks.shape[0]
    return jnp.moveaxis(blocks, 0, dim).reshape(shape)


def gathered_copies(array, axis, dim):
    blocks = from_everyone(array, axis)
    return laid_out(blocks, dim)


def sent_together(arrays, axis, dim, along):
    both = jnp.concatenate(arrays, axis=along)
    result, at, gathered = (lax.all_gather(both, axis, axis=dim, tiled=True), 0, [])
    for a in arrays:
        gathered.append(lax.slice_in_dim(result, at, at + a.shape[along], axis=along))
        at += a.shape[along]
    return tuple(gathered)


def taken_together(array, axis):
    return from_everyone(array, axis).sum(axis=0)


def taken_together_2(array, axis):
    everything = from_everyone(array, axis)
    return jnp.sum(everything.astype(jnp.float32), axis=0)


def shifted(array, axis, by):
    length = lax.axis_size(axis)
    pairs = [(i, i + by) for i in range(length) if 0 <= i + by < length]
    return lax.ppermute(array, axis, pairs)


def rotate(values, where_at):
    middle = values.shape[-1] // 2
    rates = jnp.exp(
        jnp.arange(middle, dtype=jnp.float32) * (-2.0 * math.log(THETA) / values.shape[-1])
    )
    angles = where_at.astype(jnp.float32)[..., None] * rates
    cosine = jnp.cos(angles)
    sine = jnp.sin(angles)
    first = values[..., :middle]
    second = values[..., middle:]
    return jnp.concatenate(
        [first * cosine - second * sine, second * cosine + first * sine], axis=-1
    )


def normalize(hidden, gain):
    wide = hidden.astype(jnp.float32)
    factor = lax.rsqrt(jnp.mean(wide * wide, axis=-1, keepdims=True) + EPS)
    return (wide * factor * gain).astype(jnp.bfloat16)


def attend(normed, lengths, cache, w_query, w_keyval, w_out):
    rows, drafts, width = normed.shape
    head_size = cache.shape[-1] // 2
    kv_count = cache.shape[2]
    q_count = w_query.shape[-1] // head_size
    group = q_count // kv_count
    flat = normed.reshape(rows * drafts, width)
    query = jnp.dot(flat, w_query, preferred_element_type=jnp.float32).reshape(
        rows, drafts, kv_count, group, head_size
    )
    keyval = jnp.dot(flat, w_keyval, preferred_element_type=jnp.float32).reshape(
        rows, drafts, kv_count, 2 * head_size
    )
    places = lengths[:, None] + jnp.arange(drafts, dtype=jnp.int32)[None, :]
    query = rotate(query, places[:, :, None, None]).astype(jnp.bfloat16)
    fresh_keys = rotate(keyval[..., :head_size], places[:, :, None]).astype(jnp.bfloat16)
    fresh_values = keyval[..., head_size:].astype(jnp.bfloat16)
    cached_keys = cache[..., :head_size]
    cached_values = cache[..., head_size:]
    scale = head_size ** (-0.5)
    old_scores = (
        jnp.einsum("rjkgd,rpkd->rkgjp", query, cached_keys, preferred_element_type=jnp.float32)
        * scale
    )
    live = jnp.arange(cache.shape[1], dtype=jnp.int32)[None, :] < lengths[:, None]
    old_scores = jnp.where(live[:, None, None, None, :], old_scores, NEGATIVE)
    new_scores = (
        jnp.einsum("rjkgd,rikd->rkgji", query, fresh_keys, preferred_element_type=jnp.float32)
        * scale
    )
    causal = jnp.arange(drafts)[None, :] <= jnp.arange(drafts)[:, None]
    new_scores = jnp.where(causal, new_scores, NEGATIVE)
    top = jnp.maximum(old_scores.max(axis=-1), new_scores.max(axis=-1))[..., None]
    old_weights = jnp.exp(old_scores - top)
    new_weights = jnp.exp(new_scores - top)
    total = old_weights.sum(axis=-1, keepdims=True) + new_weights.sum(axis=-1, keepdims=True)
    old_weights = (old_weights / total).astype(jnp.bfloat16)
    new_weights = (new_weights / total).astype(jnp.bfloat16)
    mixed = jnp.einsum(
        "rkgjp,rpkd->rjkgd", old_weights, cached_values, preferred_element_type=jnp.float32
    )
    mixed = mixed + jnp.einsum(
        "rkgji,rikd->rjkgd", new_weights, fresh_values, preferred_element_type=jnp.float32
    )
    heads_out = mixed.astype(jnp.bfloat16).reshape(rows * drafts, q_count * head_size)
    return jnp.dot(heads_out, w_out, preferred_element_type=jnp.float32)


def feed_forward(normed, gate_full, up_full, down_full):
    flat = normed.reshape(-1, normed.shape[-1])
    gate = jnp.dot(flat, gate_full, preferred_element_type=jnp.float32)
    up = jnp.dot(flat, up_full, preferred_element_type=jnp.float32)
    act = (jax.nn.silu(gate) * up).astype(jnp.bfloat16)
    return lax.dot_general(
        act, down_full, (((1,), (1,)), ((), ())), preferred_element_type=jnp.float32
    )


def local(
    exit_hidden,
    exit_depth,
    context_len,
    attn_gain,
    w_query,
    w_keyval,
    w_out,
    kv_cache,
    mlp_gain,
    w_gate,
    w_up,
    w_down,
):
    entry = gathered_copies(exit_hidden, ("section", "tensor"), 2)
    gate_full, up_full, down_full = sent_together((w_gate[0], w_up[0], w_down[0]), "dp", 0, 1)
    section = lax.axis_index("section")
    sections = lax.axis_size("section")
    pieces = 1
    members = R_DEV // pieces
    share = D // lax.axis_size("tensor")
    offset = lax.axis_index("tensor") * share
    entry = entry.reshape(pieces, members, DRAFT, D)
    depth = exit_depth.reshape(pieces, members)
    length = context_len.reshape(pieces, members)
    cache = kv_cache[0].reshape(pieces, members, CTX, kv_cache.shape[3], kv_cache.shape[4])
    gain = attn_gain[0]
    second_gain = mlp_gain[0]
    query_weight = w_query[0]
    keyval_weight = w_keyval[0]
    out_weight = w_out[0]

    def turn_step(turn, carry):
        received, outputs = carry
        block = turn - section
        valid = (block >= 0) & (block < pieces)
        index = jnp.clip(block, 0, pieces - 1)
        block_depth = depth[index]
        block_length = length[index]
        block_entry = entry[index]
        block_cache = cache[index]
        take = (block_depth >= section)[:, None, None]
        keep = (block_depth <= section)[:, None, None]
        active = valid & jnp.any(block_depth <= section)

        def compute(whole):
            return attend(
                normalize(whole, gain),
                block_length,
                block_cache,
                query_weight,
                keyval_weight,
                out_weight,
            )

        def branch_work(middle):
            return feed_forward(normalize(middle, second_gain), gate_full, up_full, down_full)

        def skipped(whole):
            return jnp.zeros((members * DRAFT, D), jnp.float32)

        whole = jnp.where(take, block_entry, received)
        partial_value = lax.cond(active, compute, skipped, whole)
        summed = taken_together(partial_value, "tensor").reshape(members, DRAFT, D)
        middle = (whole.astype(jnp.float32) + summed).astype(jnp.bfloat16)
        branch = lax.cond(active, branch_work, skipped, middle)
        branch_sum = (
            taken_together_2(branch.astype(jnp.bfloat16), "tensor")
            .astype(jnp.float32)
            .reshape(members, DRAFT, D)
        )
        updated = (middle.astype(jnp.float32) + branch_sum).astype(jnp.bfloat16)
        result = jnp.where(keep, updated, whole)
        own = lax.dynamic_slice_in_dim(result, offset, share, 2)
        stored = jnp.where(valid, own, outputs[index])
        outputs = lax.dynamic_update_index_in_dim(outputs, stored, index, 0)
        received = shifted(result, "section", 1)
        return (received, outputs)

    carried = D
    start = (
        jnp.zeros((members, DRAFT, carried), jnp.bfloat16),
        jnp.zeros((pieces, members, DRAFT, share), jnp.bfloat16),
    )
    final = lax.fori_loop(0, sections + pieces - 1, turn_step, start)
    return final[1]


def solution(mesh):
    in_specs = (
        P("dp", None, ("section", "tensor")),
        P("dp"),
        P("dp"),
        P("section", None),
        P("section", None, "tensor"),
        P("section", None, "tensor"),
        P("section", "tensor", None),
        P("section", "dp", None, "tensor", None),
        P("section", None),
        P("section", "dp", "tensor"),
        P("section", "dp", "tensor"),
        P("section", "dp", "tensor"),
    )
    out_specs = P("section", "dp", None, "tensor")
    return jax.shard_map(local, mesh=mesh, in_specs=in_specs, out_specs=out_specs, check_vma=False)
```

profile of v0, /device:TPU:1, one launch (start us, length us, event | category | flops | bytes accessed | tf_op | source)
XLA Modules:
  0.0 426.9 jit_solution(7864774115950235565)
XLA Ops:
  6.5 1.9 pad_maximum_fusion.1
  8.4 6.7 %copy.67 = bf16[1,2048,1024]{1,2,0:T(8,128)(2,1)} copy(bf16[1,2048,1024]{2,1,0:T(8,128)(2,1)} %param.22) | data formatting | bytes 8388608 | tf_op args[4]
  15.1 3.6 copy.70
  18.7 2.9 copy.68
  21.7 0.7 broadcast_in_dim.148
  22.4 6.5 %all-to-all-start.2 = ((bf16[4,8,4,512]{3,2,1,0:T(4,128)(2,1)}), bf16[4,8,4,512]{3,2,1,0:T(4,128)(2,1)S(1)}, u32[]{:S(2)}, u32[]{:S(2)}) async-start(bf16[4,8,4,512]{3,2,1,0:T(4,128)(2,1)} %broadcast_in_dim.148), calls=%async_computation.2 | async-start | bytes 262144 | tf_op jit(solution)/shard_map/all_to_all | solution.py:21
  28.9 0.7 compare_reduce_fusion
  29.5 4.7 %all-to-all-done.2 = bf16[4,8,4,512]{3,2,1,0:T(4,128)(2,1)S(1)} async-done(((bf16[4,8,4,512]{3,2,1,0:T(4,128)(2,1)}), bf16[4,8,4,512]{3,2,1,0:T(4,128)(2,1)S(1)}, u32[]{:S(2)}, u32[]{:S(2)}) %all-to-all-start.2) | async-done | bytes 131104 | tf_op jit(solution)/shard_map/all_to_all | solution.py:21
  34.4 253.2 %all-gather.2.cloned.1.call-done = bf16[2048,6144]{1,0:T(8,128)(2,1)} async-done(((bf16[32,6144]{1,0:T(8,128)(2,1)}), bf16[2048,6144]{1,0:T(8,128)(2,1)}) %all-gather.2.cloned.1.call-update) | async-done | bytes 25165840 | tf_op jit(solution)/shard_map/all_gather | solution.py:39
  287.6 16.8 %fusion.43 = (bf16[2048,2048]{1,0:T(8,128)(2,1)}, bf16[2048,2048]{1,0:T(8,128)(2,1)}, bf16[2048,2048]{1,0:T(8,128)(2,1)}) fusion(bf16[2048,6144]{1,0:T(8,128)(2,1)} %all-gather.2.cloned.1.call-done), kind=kLoop, calls=%fused_computation.78 | loop fusion | bytes 50331648 | tf_op jit(solution)/shard_map/slice | solution.py:41
  304.5 114.9 %while.18 = (s32[]{:T(128)}, bf16[8,4,2048]{2,1,0:T(4,128)(2,1)S(1)}, bf16[1,8,4,1024]{3,2,1,0:T(4,128)(2,1)S(1)}, s32[]{:T(128)}, s32[1,8]{1,0:T(1,128)S(1)}, /...) while((s32[]{:T(128)}, ...), condition=%wide.region_14.15_spmd, body=%wide.region_1.14_spmd.sunk | while | flops 1196084352 | bytes 66617856 | solution.py:224
  304.7 0.6 compare_bitcast_fusion.3
  306.1 0.8 broadcast_in_dim.161
  307.0 3.5 all-to-all-start
  310.5 5.4 %all-to-all-done = f32[2,32,2048]{2,1,0:T(8,128)S(1)} async-done(((f32[2,32,2048]{2,1,0:T(8,128)}), f32[2,32,2048]{2,1,0:T(8,128)S(1)}, u32[]{:S(2)}, u32[]{:S(2)}) %all-to-all-start) | async-done | bytes 524320 | tf_op jit(solution)/shard_map/while/body/eval_jaxpr/all_to_all | solution.py:21
  316.1 0.7 broadcast_in_dim.162
  316.8 3.4 all-to-all-start.1
  320.3 4.0 all-to-all-done.1
  324.6 1.3 collective-permute-start
  326.0 37.4 %collective-permute-done = bf16[8,4,2048]{2,1,0:T(4,128)(2,1)S(1)} collective-permute-done((bf16[8,4,2048]{2,1,0:T(4,128)(2,1)S(1)}, bf16[8,4,2048]{2,1,0:T(4,128)(2,1)S(1)}, u32[]{:S(2)}, u32[]{:S(2)}) %collective-permute-start) | collective-permute-done | bytes 131104 | tf_op jit(solution)/shard_map/while/body/eval_jaxpr/ppermute | solution.py:58
  363.3 0.6 compare_bitcast_fusion.3
  364.7 17.9 %conditional.4 = (f32[32,2048]{1,0:T(8,128)S(1)}) conditional(s32[]{:T(128)} %convert_element_type.171, () %tuple.76, (s32[1,8]{1,0:T(1,128)}, bf16[8,4,2048]{2,1,0:T(4,128)(2,1)S(1)}, f32[1,2048]{1,0:T(1,128)S(1)}, bf16[2048,1024]{0,1:T(8,128)(2,1)}, bf16[1,8,384,4,128]{2,4,3,1,0:T(8,128)(2,1)}, /*index=5*/bf16[2048,512]{0,1:T(8,128)(2,1)S(1)}, ...), branch_computations={%region_2.2_spmd, %region_3.8_spmd} | conditional | flops 389106816 | bytes 31677728 | solution.py:202
  364.7 0.2 fusion.12
  365.0 0.7 fusion.16
  365.7 0.7 add_convert_fusion.2
  366.7 4.4 %fusion.18 = f32[8,4,4,4,64]{4,0,3,2,1:T(8,128)S(1)} fusion(bf16[4,4,64,2048,1]{3,2,1,0,4:T(8,128)(2,1)} %bitcast.105, f32[2048]{0:T(1024)S(1)} %bitcast.110, f32[8,4]{0,1:T(4,128)S(1)} %add_rsqrt_fusion, bf16[8,4,2048]{2,1,0:T(4,128)(2,1)S(1)} %get-tuple-element.631), kind=kOutput, calls=%fused_computation.31 | convolution fusion | flops 134479872 | bytes 4464768 | tf_op jit(solution)/shard_map/while/body/eval_jaxpr/cond/branch_1_fun/dot_general | solution.py:89
  371.4 1.3 fusion.42
  372.7 0.7 iota_compare_fusion
  373.4 0.6 fusion.41
  374.0 0.3 fusion.15
  374.3 0.6 fusion.10
  375.0 1.5 copy.63
  376.6 0.4 divide_convert_fusion
  376.9 2.1 fusion.8
  379.2 0.2 fusion.9
  379.6 3.0 fusion.45
  382.6 0.8 broadcast_in_dim.161
  383.4 3.5 all-to-all-start
  386.9 5.4 %all-to-all-done = f32[2,32,2048]{2,1,0:T(8,128)S(1)} async-done(((f32[2,32,2048]{2,1,0:T(8,128)}), f32[2,32,2048]{2,1,0:T(8,128)S(1)}, u32[]{:S(2)}, u32[]{:S(2)}) %all-to-all-start) | async-done | bytes 524320 | tf_op jit(solution)/shard_map/while/body/eval_jaxpr/all_to_all | solution.py:21
  392.5 15.1 %conditional.5 = (bf16[32,2048]{1,0:T(8,128)(2,1)S(1)}) conditional(s32[]{:T(128)} %convert_element_type.171, () %tuple.75, (bf16[8,4,2048]{2,1,0:T(4,128)(2,1)S(1)}, f32[1,2048]{1,0:T(1,128)S(1)}, bf16[2048,2048]{1,0:T(8,128)(2,1)}, bf16[2048,2048]{1,0:T(8,128)(2,1)}, bf16[2048,2048]{1,0:T(8,128)(2,1)}) %tuple.78), branch_computations={%region_10.10_spmd, %region_11.12_spmd} | conditional | flops 806158336 | bytes 26747400 | solution.py:205
  392.9 4.9 %fusion.44 = f32[32,2048]{1,0:T(8,128)S(1)} fusion(bf16[32,2048]{1,0:T(8,128)(2,1)S(1)} %reshape.207, bf16[2048,2048]{1,0:T(8,128)(2,1)} %get-tuple-element.506), kind=kOutput, calls=%fused_computation.79 | convolution fusion | flops 268435456 | bytes 8781824 | tf_op jit(solution)/shard_map/while/body/eval_jaxpr/cond/branch_1_fun/dot_general | solution.py:132
  397.8 9.8 %fusion.28 = bf16[32,2048]{1,0:T(8,128)(2,1)S(1)} fusion(bf16[2048,2048]{1,0:T(8,128)(2,1)} %get-tuple-element.508, bf16[32,2048]{1,0:T(8,128)(2,1)S(1)} %reshape.207, bf16[2048,2048]{1,0:T(8,128)(2,1)} %get-tuple-element.507, f32[32,2048]{1,0:T(8,128)S(1)} %fusion.44), kind=kOutput, calls=%fused_computation.51 | convolution fusion | flops 537264128 | bytes 17301504 | tf_op jit(solution)/shard_map/while/body/eval_jaxpr/cond/branch_1_fun/dot_general | solution.py:135
  407.7 0.7 broadcast_in_dim.162
  408.4 3.4 all-to-all-start.1
  411.8 4.0 all-to-all-done.1
  416.1 1.3 collective-permute-start
  417.5 1.9 collective-permute-done
  419.4 0.6 copy-done.3
  (67 shorter events, 3.1 us)
Async XLA Ops:
  6.5 281.1 %all-gather.2.cloned.1.call-start = ((), (), s32[]{:S(2)}) async-start(), calls=%async_computation.3 | async-start | bytes 25559040 | tf_op jit(solution)/shard_map/all_gather | solution.py:39
  8.4 6.7 %copy-start.1 = (bf16[1,8,384,4,128]{4,3,2,1,0:T(4,128)(2,1)S(1)}, bf16[1,8,384,4,128]{4,3,2,1,0:T(4,128)(2,1)}, u32[]{:S(2)}) copy-start(bf16[1,8,384,4,128]{4,3,2,1,0:T(4,128)(2,1)} %param.25) | copy-start | bytes 9437188
  15.1 6.6 %copy-start.7 = (bf16[8,4,512]{2,1,0:T(4,128)(2,1)S(1)}, bf16[8,4,512]{2,1,0:T(4,128)(2,1)}, u32[]{:S(2)}) copy-start(bf16[8,4,512]{2,1,0:T(4,128)(2,1)} %param.18) | copy-start | bytes 98308
  15.1 13.7 %copy-start.8 = (s32[8]{0:T(128)S(1)}, s32[8]{0:T(128)}, u32[]{:S(2)}) copy-start(s32[8]{0:T(128)} %param.19) | copy-start | bytes 100
  22.4 11.8 %all-to-all-start.2 = ((bf16[4,8,4,512]{3,2,1,0:T(4,128)(2,1)}), bf16[4,8,4,512]{3,2,1,0:T(4,128)(2,1)S(1)}, u32[]{:S(2)}, u32[]{:S(2)}) async-start(bf16[4,8,4,512]{3,2,1,0:T(4,128)(2,1)} %broadcast_in_dim.148), calls=%async_computation.2 | async-start | bytes 262144 | tf_op jit(solution)/shard_map/all_to_all | solution.py:21
  34.4 270.1 %copy-start.4 = (f32[1,2048]{1,0:T(1,128)S(1)}, f32[1,2048]{1,0:T(1,128)}, u32[]{:S(2)}) copy-start(f32[1,2048]{1,0:T(1,128)} %param.21) | copy-start | bytes 24580
  34.4 270.1 %copy-start.5 = (f32[1,2048]{1,0:T(1,128)S(1)}, f32[1,2048]{1,0:T(1,128)}, u32[]{:S(2)}) copy-start(f32[1,2048]{1,0:T(1,128)} %param.26) | copy-start | bytes 24580
  307.0 8.9 %all-to-all-start = ((f32[2,32,2048]{2,1,0:T(8,128)}), f32[2,32,2048]{2,1,0:T(8,128)S(1)}, u32[]{:S(2)}, u32[]{:S(2)}) async-start(f32[2,32,2048]{2,1,0:T(8,128)} %broadcast_in_dim.161), calls=%async_computation | async-start | bytes 1048576 | tf_op jit(solution)/shard_map/while/body/eval_jaxpr/all_to_all | solution.py:21
  316.1 8.4 %copy-start.6 = (pred[8]{0:T(512)(128)(4,1)S(1)}, pred[8]{0:T(512)(128)(4,1)}, u32[]{:S(2)}) copy-start(pred[8]{0:T(512)(128)(4,1)} %get-tuple-element.818) | copy-start | bytes 28 | tf_op jit(solution)/shard_map/while
  316.1 47.3 %copy-start.9 = (s32[8]{0:T(128)S(1)}, s32[8]{0:T(128)}, u32[]{:S(2)}) copy-start(s32[8]{0:T(128)} %get-tuple-element.935) | copy-start | bytes 100 | tf_op jit(solution)/shard_map/while
  316.8 7.5 %all-to-all-start.1 = ((bf16[2,32,2048]{2,1,0:T(8,128)(2,1)}), bf16[2,32,2048]{2,1,0:T(8,128)(2,1)S(1)}, u32[]{:S(2)}, u32[]{:S(2)}) async-start(bf16[2,32,2048]{2,1,0:T(8,128)(2,1)} %broadcast_in_dim.162), calls=%async_computation.1 | async-start | bytes 524288 | tf_op jit(solution)/shard_map/while/body/eval_jaxpr/all_to_all | solution.py:21
  324.6 38.7 %collective-permute-start = (bf16[8,4,2048]{2,1,0:T(4,128)(2,1)S(1)}, bf16[8,4,2048]{2,1,0:T(4,128)(2,1)S(1)}, u32[]{:S(2)}, u32[]{:S(2)}) collective-permute-start(bf16[8,4,2048]{2,1,0:T(4,128)(2,1)S(1)} %fusion.58), channel_id=1, source_target_pairs={{0,128},{1,129},{2,130},{3,131},{4,132},{5,133},{6,134},{7,135},{8... | collective-permute-start | bytes 393224 | tf_op jit(solution)/shard_map/while/body/eval_jaxpr/ppermute | solution.py:58
  366.7 6.7 %copy-start.2 = (bf16[1,8,384,4,128]{2,4,3,1,0:T(8,128)(2,1)S(1)}, bf16[1,8,384,4,128]{2,4,3,1,0:T(8,128)(2,1)}, u32[]{:S(2)}) copy-start(bf16[1,8,384,4,128]{2,4,3,1,0:T(8,128)(2,1)} %get-tuple-element.501) | copy-start | bytes 9437188 | tf_op jit(solution)/shard_map/while/body/eval_jaxpr/cond
  376.6 2.6 copy-start
  383.4 8.9 %all-to-all-start = ((f32[2,32,2048]{2,1,0:T(8,128)}), f32[2,32,2048]{2,1,0:T(8,128)S(1)}, u32[]{:S(2)}, u32[]{:S(2)}) async-start(f32[2,32,2048]{2,1,0:T(8,128)} %broadcast_in_dim.161), calls=%async_computation | async-start | bytes 1048576 | tf_op jit(solution)/shard_map/while/body/eval_jaxpr/all_to_all | solution.py:21
  392.5 23.4 %copy-start.6 = (pred[8]{0:T(512)(128)(4,1)S(1)}, pred[8]{0:T(512)(128)(4,1)}, u32[]{:S(2)}) copy-start(pred[8]{0:T(512)(128)(4,1)} %get-tuple-element.818) | copy-start | bytes 28 | tf_op jit(solution)/shard_map/while
  392.5 26.8 %copy-start.9 = (s32[8]{0:T(128)S(1)}, s32[8]{0:T(128)}, u32[]{:S(2)}) copy-start(s32[8]{0:T(128)} %get-tuple-element.935) | copy-start | bytes 100 | tf_op jit(solution)/shard_map/while
  408.4 7.5 %all-to-all-start.1 = ((bf16[2,32,2048]{2,1,0:T(8,128)(2,1)}), bf16[2,32,2048]{2,1,0:T(8,128)(2,1)S(1)}, u32[]{:S(2)}, u32[]{:S(2)}) async-start(bf16[2,32,2048]{2,1,0:T(8,128)(2,1)} %broadcast_in_dim.162), calls=%async_computation.1 | async-start | bytes 524288 | tf_op jit(solution)/shard_map/while/body/eval_jaxpr/all_to_all | solution.py:21
  416.1 3.2 collective-permute-start
  419.4 0.6 copy-start.3
Sparse Core Ops, SparseCore 0:
  10.9 276.7 all-gather.1
where the time goes:
time: 428 us; the launch traced here: 427 us
  waiting for transfers between devices  316 us (74%)
  local copies, waits for them, and re-layouts  36.9 us (9%)
  matrix products  27 us (6%)
  starting transfers between devices  22.9 us (5%)
  between operations  13.5 us (3%)
  other arithmetic  8.61 us (2%)
    all_gather x1, waiting for transfers between devices, sent_together(): lax.all_gather(both, axis, axis=dim, tiled=True)  253 us
    ppermute x2, waiting for transfers between devices, shifted(): return lax.ppermute(array, axis, pairs)  39.3 us
    all_to_all x5, waiting for transfers between devices, from_everyone(): lax.all_to_all(jnp.broadcast_to(array[None], (length, *array.shape)), axi...  23.5 us
    all_to_all x5, starting transfers between devices, from_everyone(): lax.all_to_all(jnp.broadcast_to(array[None], (length, *array.shape)), axi...  20.4 us
    slice x1, local copies, waits for them, and re-layouts, sent_together(): lax.slice_in_dim(result, at, at + a.shape[along], axis=along)  16.8 us
    unnamed x14, local copies, waits for them, and re-layouts  10.3 us
    dot_general x1, matrix products, feed_forward(): lax.dot_general(act, down_full, (((1,), (1,)), ((), ())), preferred_eleme...  9.81 us
  transfers between devices with their start and end apart: 8, of which 8 were waited for; matrix products, arithmetic and copies ran while one was open for 3% of the time, Pallas kernels for 0%

commit v1 on v0

v1 whole, which is shorter than its diff:
```python
import math

import jax
import jax.numpy as jnp
from jax import lax
from jax.experimental import pallas as pl
from jax.experimental.pallas import tpu as pltpu
from jax.sharding import Mesh, PartitionSpec as P

D = 2048
DRAFT = 4
CTX = 384
ROWS = 8
TOKENS = ROWS * DRAFT
HD = 64
QH = 16
KH = 4
SLOTS = CTX * KH
VMEM_LIMIT = 60 * 1024 * 1024
FFS = 256
EPS = 1e-05
THETA = 500000.0
NEGATIVE = -1e30
PLANE = ("tensor", "y", "xh")
CHIP = ("section", "tensor")
Z = 8


def attend_kernel(
    lens, hidden, gain, cosine, sine, wq_h, wkv_h, wo_h, kv_h, out, wq, wkv, wo, kv, qs, nk, hs, bias, sems
):
    pieces = 4
    step = D // pieces
    copies = []
    for p in range(pieces):
        at = pl.ds(p * step, step)
        copies.append(pltpu.make_async_copy(wq_h.at[at], wq.at[at], sems.at[2 * p]))
        copies.append(pltpu.make_async_copy(wkv_h.at[at], wkv.at[at], sems.at[2 * p + 1]))
    base = 2 * pieces
    kv_copies = [
        pltpu.make_async_copy(kv_h.at[r], kv.at[r], sems.at[base + r]) for r in range(ROWS)
    ]
    wo_copy = pltpu.make_async_copy(wo_h, wo, sems.at[base + ROWS])
    for c in copies + kv_copies + [wo_copy]:
        c.start()

    row = lax.broadcasted_iota(jnp.int32, (4 * QH, SLOTS), 0)
    place = lax.broadcasted_iota(jnp.int32, (4 * QH, SLOTS), 1)
    bias[...] = jnp.where((place & 3) == (row >> 4), 0.0, NEGATIVE)
    new_row = lax.broadcasted_iota(jnp.int32, (4 * QH, DRAFT * KH), 0)
    new_col = lax.broadcasted_iota(jnp.int32, (4 * QH, DRAFT * KH), 1)
    seen = ((new_col & 3) == (new_row >> 4)) & ((new_col >> 2) <= (new_row & 3))

    wide = hidden[...].astype(jnp.float32)
    factor = lax.rsqrt(jnp.mean(wide * wide, axis=-1, keepdims=True) + EPS)
    normed = (wide * factor * gain[...]).astype(jnp.bfloat16)
    q = jnp.zeros((TOKENS, QH * HD), jnp.float32)
    new = jnp.zeros((TOKENS, KH * 2 * HD), jnp.float32)
    for p in range(pieces):
        at = pl.ds(p * step, step)
        copies[2 * p].wait()
        copies[2 * p + 1].wait()
        part = normed[:, p * step : (p + 1) * step]
        q = q + jnp.dot(part, wq[at], preferred_element_type=jnp.float32)
        new = new + jnp.dot(part, wkv[at], preferred_element_type=jnp.float32)

    lane = lax.broadcasted_iota(jnp.int32, (TOKENS, 128), 1)
    low = (lane & 63) < 32
    left = lane < HD
    cos_all = cosine[...]
    sin_all = sine[...]

    def turned(block, c, s):
        other = jnp.where(low, pltpu.roll(block, 96, 1), pltpu.roll(block, 32, 1))
        return block * c + other * s

    scale = HD ** (-0.5)
    for m in range(QH // 2):
        block = turned(q[:, m * 128 : (m + 1) * 128], cos_all, sin_all) * scale
        pair = (jnp.where(left, block, 0.0), jnp.where(left, pltpu.roll(block, HD, 1), 0.0))
        for half in range(2):
            for j in range(DRAFT):
                at = ((2 * m + half) * DRAFT + j) * ROWS
                qs[at : at + ROWS, :] = pair[half][j * ROWS : (j + 1) * ROWS, :]
    key_cos = jnp.where(left, cos_all, 1.0)
    key_sin = jnp.where(left, sin_all, 0.0)
    for h in range(KH):
        block = turned(new[:, h * 128 : (h + 1) * 128], key_cos, key_sin)
        for i in range(DRAFT):
            at = (i * KH + h) * ROWS
            nk[at : at + ROWS, :] = block[i * ROWS : (i + 1) * ROWS, :]

    last = (((1,), (1,)), ((), ()))
    for r in range(ROWS):
        fresh = nk[pl.ds(r, DRAFT * KH, stride=ROWS), :].astype(jnp.bfloat16)
        mine = qs[pl.ds(r, 4 * QH, stride=ROWS), :].astype(jnp.bfloat16)
        kv_copies[r].wait()
        stored = kv[r]
        scores = lax.dot_general(mine, stored, last, preferred_element_type=jnp.float32)
        scores = jnp.where(place < KH * lens[r], scores, NEGATIVE) + bias[...]
        new_scores = lax.dot_general(mine, fresh, last, preferred_element_type=jnp.float32)
        new_scores = jnp.where(seen, new_scores, NEGATIVE)
        top = jnp.maximum(
            jnp.max(scores, axis=-1, keepdims=True), jnp.max(new_scores, axis=-1, keepdims=True)
        )
        weights = jnp.exp(scores - top)
        new_weights = jnp.exp(new_scores - top)
        total = jnp.sum(weights, axis=-1, keepdims=True) + jnp.sum(
            new_weights, axis=-1, keepdims=True
        )
        mixed = jnp.dot(
            weights.astype(jnp.bfloat16), stored, preferred_element_type=jnp.float32
        ) + jnp.dot(new_weights.astype(jnp.bfloat16), fresh, preferred_element_type=jnp.float32)
        hs[pl.ds(r, 4 * QH, stride=ROWS), :] = mixed / total

    side = lax.broadcasted_iota(jnp.int32, (ROWS, 128), 1) < HD
    rows = []
    for j in range(DRAFT):
        tiles = []
        for m in range(QH // 2):
            first = ((2 * m) * DRAFT + j) * ROWS
            second = ((2 * m + 1) * DRAFT + j) * ROWS
            tiles.append(
                jnp.where(
                    side, pltpu.roll(hs[first : first + ROWS, :], HD, 1), hs[second : second + ROWS, :]
                )
            )
        rows.append(jnp.concatenate(tiles, axis=1))
    heads = jnp.concatenate(rows, axis=0).astype(jnp.bfloat16)
    wo_copy.wait()
    result = jnp.dot(heads, wo[...], preferred_element_type=jnp.float32)
    for j in range(DRAFT):
        out[j] = result[j * ROWS : (j + 1) * ROWS, :].astype(jnp.bfloat16)


def attend(lens, hidden, gain, cosine, sine, wq, wkv, wo, kv):
    hbm = pl.BlockSpec(memory_space=pltpu.HBM)
    vmem = pl.BlockSpec(memory_space=pltpu.VMEM)
    return pl.pallas_call(
        attend_kernel,
        out_shape=jax.ShapeDtypeStruct((DRAFT, ROWS, D), jnp.bfloat16),
        in_specs=[pl.BlockSpec(memory_space=pltpu.SMEM)] + [vmem] * 4 + [hbm] * 4,
        out_specs=vmem,
        scratch_shapes=[
            pltpu.VMEM((D, QH * HD), jnp.bfloat16),
            pltpu.VMEM((D, KH * 2 * HD), jnp.bfloat16),
            pltpu.VMEM((QH * HD, D), jnp.bfloat16),
            pltpu.VMEM((ROWS, SLOTS, 128), jnp.bfloat16),
            pltpu.VMEM((4 * QH * ROWS, 128), jnp.float32),
            pltpu.VMEM((DRAFT * KH * ROWS, 128), jnp.float32),
            pltpu.VMEM((4 * QH * ROWS, 128), jnp.float32),
            pltpu.VMEM((4 * QH, SLOTS), jnp.float32),
            pltpu.SemaphoreType.DMA((17,)),
        ],
        compiler_params=pltpu.CompilerParams(vmem_limit_bytes=VMEM_LIMIT),
        cost_estimate=pl.CostEstimate(flops=400_000_000, transcendentals=800_000, bytes_accessed=13_500_000),
        name="attend",
    )(lens, hidden, gain, cosine, sine, wq, wkv, wo, kv)


def mlp_kernel(tokens, gathered, out, weights, sems):
    copies = [
        pltpu.make_async_copy(gathered.at[h, z], weights.at[z, :, h], sems.at[2 * z + h])
        for z in range(Z)
        for h in range(2)
    ]
    for c in copies:
        c.start()
    count = tokens.shape[0]
    gate = jnp.zeros((count, FFS), jnp.float32)
    up = jnp.zeros((count, FFS), jnp.float32)
    for z in range(Z):
        copies[2 * z].wait()
        copies[2 * z + 1].wait()
        part = tokens[:, z * 256 : (z + 1) * 256]
        gate = gate + jnp.dot(
            part, weights[z, :, :, 0:16, :].reshape(256, FFS), preferred_element_type=jnp.float32
        )
        up = up + jnp.dot(
            part, weights[z, :, :, 16:32, :].reshape(256, FFS), preferred_element_type=jnp.float32
        )
    act = (gate / (1.0 + jnp.exp(-gate)) * up).astype(jnp.bfloat16)
    for z in range(Z):
        down = weights[z, :, :, 32:48, :].reshape(256, FFS)
        out[:, z * 256 : (z + 1) * 256] = lax.dot_general(
            act, down, (((1,), (1,)), ((), ())), preferred_element_type=jnp.float32
        ).astype(jnp.bfloat16)


def mlp(tokens, gathered):
    vmem = pl.BlockSpec(memory_space=pltpu.VMEM)
    return pl.pallas_call(
        mlp_kernel,
        out_shape=jax.ShapeDtypeStruct(tokens.shape, jnp.bfloat16),
        in_specs=[vmem, pl.BlockSpec(memory_space=pltpu.HBM)],
        out_specs=vmem,
        scratch_shapes=[
            pltpu.VMEM((Z, 8, 2, 48, FFS), jnp.bfloat16),
            pltpu.SemaphoreType.DMA((2 * Z,)),
        ],
        compiler_params=pltpu.CompilerParams(vmem_limit_bytes=VMEM_LIMIT),
        cost_estimate=pl.CostEstimate(flops=400_000_000, transcendentals=32768, bytes_accessed=4_200_000),
        name="mlp",
    )(tokens, gathered)


def after(first, then):
    return lax.optimization_barrier((first, then))[1]


def normalize(hidden, gain):
    wide = hidden.astype(jnp.float32)
    factor = lax.rsqrt(jnp.mean(wide * wide, axis=-1, keepdims=True) + EPS)
    return (wide * factor * gain).astype(jnp.bfloat16)


def local(
    exit_hidden,
    exit_depth,
    context_len,
    attn_gain,
    w_query,
    w_keyval,
    w_out,
    kv_cache,
    mlp_gain,
    w_gate,
    w_up,
    w_down,
):
    section = lax.axis_index("section")
    tensor = lax.axis_index("tensor")

    rows = jnp.stack([w_gate[0], w_up[0], w_down[0]])
    sliced = rows.reshape(3, 2, 16, 8, FFS).transpose(1, 3, 0, 2, 4).reshape(16, 48, FFS)
    blocks = lax.all_to_all(sliced, ("section", "y", "xh"), 0, 0, tiled=True)
    blocks = blocks.reshape(2, 8, 48, FFS)

    def gathered(block):
        return lax.all_gather(block, ("section", "z"), axis=0).reshape(2, Z, 8, 48, FFS)

    weights = [gathered(blocks[0])]

    mine = exit_hidden.transpose(1, 0, 2).reshape(TOKENS, 512)
    entry = lax.all_to_all(
        jnp.broadcast_to(mine[None], (4, TOKENS, 512)), CHIP, 0, 0, tiled=True
    )
    whole = entry.transpose(1, 0, 2).reshape(TOKENS, D)

    where_at = (jnp.arange(DRAFT, dtype=jnp.int32)[:, None] + context_len[None, :]).reshape(TOKENS)
    rates = jnp.exp(jnp.arange(HD // 2, dtype=jnp.float32) * (-2.0 * math.log(THETA) / HD))
    angles = where_at.astype(jnp.float32)[:, None] * rates
    c = jnp.cos(angles)
    s = jnp.sin(angles)
    cosine = jnp.concatenate([c, c, c, c], axis=1)
    sine = jnp.concatenate([-s, s, -s, s], axis=1)

    cache = kv_cache[0].reshape(ROWS, SLOTS, 128)
    other_gain = lax.ppermute(mlp_gain, "section", [(0, 1), (1, 0)])
    gains = [jnp.where(section == l, mlp_gain, other_gain) for l in range(2)]

    piece = section * 2 + tensor
    kept = lax.dynamic_slice_in_dim(whole, piece * ROWS, ROWS, 0)
    states = []
    for l in range(2):
        partial = attend(
            context_len, whole, attn_gain, cosine, sine, w_query[0], w_keyval[0], w_out[0], cache
        )
        parts = lax.all_to_all(partial, CHIP, 0, 0, tiled=True)
        mid = (
            kept.astype(jnp.float32)
            + parts[2 * l].astype(jnp.float32)
            + parts[2 * l + 1].astype(jnp.float32)
        ).astype(jnp.bfloat16)
        if l == 0:
            weights.append(gathered(after(mid, blocks[1])))
        mlp_in = normalize(mid, gains[l])
        everyone = lax.all_to_all(
            jnp.broadcast_to(mlp_in[None], (16, ROWS, D)), PLANE, 0, 0, tiled=True
        )
        share = mlp(everyone.reshape(16 * ROWS, D), weights[l])
        shares = lax.all_to_all(share.reshape(16, ROWS, D), PLANE, 0, 0, tiled=True)
        updated = (mid.astype(jnp.float32) + jnp.sum(shares.astype(jnp.float32), axis=0)).astype(
            jnp.bfloat16
        )
        kept = jnp.where((exit_depth <= l)[:, None], updated, kept)
        if l == 0:
            spread = lax.all_to_all(
                jnp.broadcast_to(kept[None], (4, ROWS, D)), CHIP, 0, 0, tiled=True
            )
            whole = spread.reshape(TOKENS, D)
            states.append(
                lax.dynamic_slice_in_dim(spread, tensor * (D // 2), D // 2, 2)
            )
        else:
            halves = kept.reshape(ROWS, 2, D // 2).transpose(1, 0, 2)
            spread = lax.all_to_all(
                jnp.concatenate([halves, halves]), CHIP, 0, 0, tiled=True
            )
            states.append(spread)
    result = jnp.where(section == 0, states[0], states[1])
    return result.transpose(1, 0, 2)[None]


def solution(mesh):
    wide = Mesh(mesh.devices.reshape(2, 2, Z, 4, 2), ("section", "tensor", "z", "y", "xh"))
    dp = ("z", "y", "xh")
    in_specs = (
        P(dp, None, ("section", "tensor")),
        P(dp),
        P(dp),
        P("section", None),
        P("section", None, "tensor"),
        P("section", None, "tensor"),
        P("section", "tensor", None),
        P("section", dp, None, "tensor", None),
        P("section", None),
        P("section", dp, "tensor"),
        P("section", dp, "tensor"),
        P("section", dp, "tensor"),
    )
    out_specs = P("section", dp, None, "tensor")
    return jax.shard_map(local, mesh=wide, in_specs=in_specs, out_specs=out_specs, check_vma=False)
```

time: 428 us -> 167 us (0.39)
  waiting for transfers between devices: 316 us -> 28.4 us
  blocking collectives: 0 us -> 61.4 us
  local copies, waits for them, and re-layouts: 36.9 us -> 4.76 us
  Pallas kernels: 0 us -> 30.4 us
  matrix products: 27 us -> 0 us
  other arithmetic: 8.61 us -> 3.39 us
    all_gather x1 -> x2, waiting for transfers between devices: 253 us -> 0.02 us  [gathered(): lax.all_gather(block, ('section', 'z'), axis=0).reshape(2, Z, 8, 48, FFS)]
    all_to_all x0 -> x5, blocking collectives: none -> 61.4 us  [the longest x1 17.2 us: local(): blocks = lax.all_to_all(sliced, ('section', 'y', 'xh'), 0, 0, tiled=True)]
    ppermute x2 -> x1, waiting for transfers between devices: 39.3 us -> 0.83 us  [local(): other_gain = lax.ppermute(mlp_gain, 'section', [(0, 1), (1, 0)])]
    pallas_call x0 -> x4, Pallas kernels: none -> 30.4 us  [the longest x2 21.4 us: attend(): pl.pallas_call(attend_kernel, out_shape=jax.ShapeDtypeStruct((DRAFT, ROWS...]
    dot_general x9 -> x0, matrix products: 27 us -> none  [the longest x1 9.81 us: feed_forward(): lax.dot_general(act, down_full, (((1,), (1,)), ((), ())), preferred_eleme...]
    slice x2 -> x1, local copies, waits for them, and re-layouts: 16.9 us -> 0.79 us  [local(): weights.append(gathered(after(mid, blocks[1])))]
    unnamed x14 -> x16, local copies, waits for them, and re-layouts: 10.3 us -> 0.91 us
  transfers between devices with their start and end apart: 8 -> 8, of which waited for: 8 -> 6; matrix products, arithmetic and copies ran while one was open for 3% -> 2% of each run, Pallas kernels for 0% -> 16%
where the time goes in v1:
time: 167 us; the launch traced here: 166 us
  blocking collectives  61.4 us (37%)
  Pallas kernels  30.4 us (18%)
  waiting for transfers between devices  28.4 us (17%)
  starting transfers between devices  24 us (14%)
  between operations  13.6 us (8%)
  local copies, waits for them, and re-layouts  4.76 us (3%)
  other arithmetic  3.39 us (2%)
    pallas_call x2, Pallas kernels, attend(): pl.pallas_call(attend_kernel, out_shape=jax.ShapeDtypeStruct((DRAFT, ROWS...  21.4 us
    all_to_all x1, blocking collectives, local(): blocks = lax.all_to_all(sliced, ('section', 'y', 'xh'), 0, 0, tiled=True)  17.2 us
    all_to_all x1, blocking collectives, local(): lax.all_to_all(jnp.broadcast_to(mlp_in[None], (16, ROWS, D)), PLANE, 0, 0...  13.2 us
    all_to_all x1, blocking collectives, local(): shares = lax.all_to_all(share.reshape(16, ROWS, D), PLANE, 0, 0, tiled=True)  13 us
    all_to_all x1, blocking collectives, local(): lax.all_to_all(jnp.broadcast_to(kept[None], (4, ROWS, D)), CHIP, 0, 0, ti...  10.3 us
    all_to_all x1, waiting for transfers between devices, local(): lax.all_to_all(jnp.broadcast_to(mlp_in[None], (16, ROWS, D)), PLANE, 0, 0...  9.03 us
    pallas_call x2, Pallas kernels, mlp(): pl.pallas_call(mlp_kernel, out_shape=jax.ShapeDtypeStruct(tokens.shape, j...  8.96 us
    all_to_all x1, waiting for transfers between devices, local(): shares = lax.all_to_all(share.reshape(16, ROWS, D), PLANE, 0, 0, tiled=True)  8.64 us
  transfers between devices with their start and end apart: 8, of which 6 were waited for; matrix products, arithmetic and copies ran while one was open for 2% of the time, Pallas kernels for 16%

profile of v1, /device:TPU:1, one launch (start us, length us, event | category | flops | bytes accessed | tf_op | source)
XLA Modules:
  0.0 165.9 jit_solution(6478612342494970185)
XLA Ops:
  6.5 0.0 all-gather.5.cloned.1.call-start
  6.5 1.1 pad_maximum_fusion
  7.6 0.1 copy.25
  7.7 0.1 copy.22
  7.8 17.2 %all_to_all.50 = bf16[16,48,256]{2,1,0:T(8,128)(2,1)S(1)} all-to-all(bf16[16,48,256]{2,1,0:T(8,128)(2,1)S(1)} %bitcast.74), channel_id=1, replica_groups=mesh['section'=2,'tensor'=2,'z'=8,'y'=4,'xh'=2] {'section','y','xh'}, dimensions={0} | all-to-all | bytes 786432 | tf_op jit(solution)/shard_map/all_to_all | solution.py:236
  25.1 0.8 fusion.15
  25.8 0.0 all-gather.5.cloned.1.call-update
  25.9 0.7 broadcast_in_dim.27
  26.6 5.1 %all-to-all-start = ((bf16[4,32,512]{2,1,0:T(8,128)(2,1)}), bf16[4,32,512]{2,1,0:T(8,128)(2,1)S(1)}, u32[]{:S(2)}, u32[]{:S(2)}) async-start(bf16[4,32,512]{2,1,0:T(8,128)(2,1)} %broadcast_in_dim.27), calls=%async_computation | async-start | bytes 262144 | tf_op jit(solution)/shard_map/all_to_all | solution.py:245
  31.6 0.1 convert_element_type.74
  31.7 0.1 fusion.12
  31.9 0.7 pad_maximum_fusion.2
  32.6 2.6 %all-to-all-done = bf16[4,32,512]{2,1,0:T(8,128)(2,1)S(1)} async-done(((bf16[4,32,512]{2,1,0:T(8,128)(2,1)}), bf16[4,32,512]{2,1,0:T(8,128)(2,1)S(1)}, u32[]{:S(2)}, u32[]{:S(2)}) %all-to-all-start) | async-done | bytes 131104 | tf_op jit(solution)/shard_map/all_to_all | solution.py:245
  35.2 0.7 copy.24
  35.9 10.7 %attend.2 = bf16[4,8,2048]{2,1,0:T(8,128)(2,1)} custom-call(s32[8]{0:T(128)} %lens.3, bf16[32,2048]{1,0:T(8,128)(2,1)} %bitcast.77, f32[1,2048]{1,0:T(1,128)} %gain.3, f32[32,128]{1,0:T(8,128)} %get-tuple-element.20.cosine, f32[32,128]{1,0:T(8,128)} %get-tuple-element.21.sine, bf16[2048,1024]{1,0:T(8,128)(2,1)} %bitcast.59, bf16[2048,512]{1,0:T(8,128)(2,1)} %bitcast.65, ...), custom_call_target="tpu_custom_call" | custom-call | flops 400000000 | bytes 13500000 | tf_op jit(solution)/shard_map/attend/pallas_call | solution.py:139
  46.6 4.3 %all-to-all-start.1 = ((bf16[4,8,2048]{2,1,0:T(8,128)(2,1)}), bf16[4,8,2048]{2,1,0:T(8,128)(2,1)S(1)}, u32[]{:S(2)}, u32[]{:S(2)}) async-start(bf16[4,8,2048]{2,1,0:T(8,128)(2,1)} %attend.2), calls=%async_computation.1 | async-start | bytes 262144 | tf_op jit(solution)/shard_map/all_to_all | solution.py:269
  50.9 3.9 %all-to-all-done.1 = bf16[4,8,2048]{2,1,0:T(8,128)(2,1)S(1)} async-done(((bf16[4,8,2048]{2,1,0:T(8,128)(2,1)}), bf16[4,8,2048]{2,1,0:T(8,128)(2,1)S(1)}, u32[]{:S(2)}, u32[]{:S(2)}) %all-to-all-start.1) | async-done | bytes 131104 | tf_op jit(solution)/shard_map/all_to_all | solution.py:269
  54.8 0.1 fusion
  54.9 0.0 all-gather.7.cloned.1.call-update
  55.0 0.7 collective-permute-start
  55.7 0.8 collective-permute-done
  56.6 0.1 fusion.2
  56.7 0.0 copy-start.6
  56.7 13.2 %all_to_all.51 = bf16[16,8,2048]{2,1,0:T(8,128)(2,1)} all-to-all(bf16[16,8,2048]{2,1,0:T(8,128)(2,1)S(1)} %broadcast_in_dim.28), channel_id=1, replica_groups=mesh['section'=2,'tensor'=2,'z'=8,'y'=4,'xh'=2] {'tensor','y','xh'}, dimensions={0} | all-to-all | bytes 1048576 | tf_op jit(solution)/shard_map/all_to_all | solution.py:278
  70.0 4.5 %mlp.2 = bf16[128,2048]{1,0:T(8,128)(2,1)} custom-call(bf16[128,2048]{1,0:T(8,128)(2,1)} %bitcast.71, bf16[2,8,8,48,256]{4,3,2,1,0:T(8,128)(2,1)} %bitcast.67), custom_call_target="tpu_custom_call" | custom-call | flops 400000000 | bytes 4200000 | tf_op jit(solution)/shard_map/mlp/pallas_call | solution.py:192
  74.4 3.9 %all-to-all-start.4 = ((bf16[16,8,2048]{2,1,0:T(8,128)(2,1)}), bf16[16,8,2048]{2,1,0:T(8,128)(2,1)S(1)}, u32[]{:S(2)}, u32[]{:S(2)}) async-start(bf16[16,8,2048]{2,1,0:T(8,128)(2,1)} %bitcast.70), calls=%async_computation.4 | async-start | bytes 1048576 | tf_op jit(solution)/shard_map/all_to_all | solution.py:282
  78.3 8.6 %all-to-all-done.4 = bf16[16,8,2048]{2,1,0:T(8,128)(2,1)S(1)} async-done(((bf16[16,8,2048]{2,1,0:T(8,128)(2,1)}), bf16[16,8,2048]{2,1,0:T(8,128)(2,1)S(1)}, u32[]{:S(2)}, u32[]{:S(2)}) %all-to-all-start.4) | async-done | bytes 524320 | tf_op jit(solution)/shard_map/all_to_all | solution.py:282
  87.0 0.1 convert_reduce_fusion.1
  87.1 0.1 fusion.11
  87.2 10.3 %all_to_all.52 = bf16[4,8,2048]{2,1,0:T(8,128)(2,1)} all-to-all(bf16[4,8,2048]{2,1,0:T(8,128)(2,1)S(1)} %broadcast_in_dim.29), channel_id=1, replica_groups=mesh['section'=2,'tensor'=2,'z'=8,'y'=4,'xh'=2] {'section','tensor'}, dimensions={0} | all-to-all | bytes 262144 | tf_op jit(solution)/shard_map/all_to_all | solution.py:288
  97.4 10.7 %attend.3 = bf16[4,8,2048]{2,1,0:T(8,128)(2,1)} custom-call(s32[8]{0:T(128)} %lens.3, bf16[32,2048]{1,0:T(8,128)(2,1)} %bitcast.76, f32[1,2048]{1,0:T(1,128)} %gain.3, f32[32,128]{1,0:T(8,128)} %get-tuple-element.20.cosine, f32[32,128]{1,0:T(8,128)} %get-tuple-element.21.sine, bf16[2048,1024]{1,0:T(8,128)(2,1)} %bitcast.60, bf16[2048,512]{1,0:T(8,128)(2,1)} %bitcast.66, ...), custom_call_target="tpu_custom_call" | custom-call | flops 400000000 | bytes 13500000 | tf_op jit(solution)/shard_map/attend/pallas_call | solution.py:139
  108.1 7.6 %all_to_all.53 = bf16[4,8,2048]{2,1,0:T(8,128)(2,1)S(1)} all-to-all(bf16[4,8,2048]{2,1,0:T(8,128)(2,1)} %attend.3), channel_id=1, replica_groups=mesh['section'=2,'tensor'=2,'z'=8,'y'=4,'xh'=2] {'section','tensor'}, dimensions={0} | all-to-all | bytes 262144 | tf_op jit(solution)/shard_map/all_to_all | solution.py:269
  115.7 0.1 fusion.4
  115.9 0.1 fusion.6
  115.9 0.9 broadcast_in_dim.55
  116.8 3.6 %all-to-all-start.7 = ((bf16[16,8,2048]{2,1,0:T(8,128)(2,1)}), bf16[16,8,2048]{2,1,0:T(8,128)(2,1)S(1)}, u32[]{:S(2)}, u32[]{:S(2)}) async-start(bf16[16,8,2048]{2,1,0:T(8,128)(2,1)} %broadcast_in_dim.55), calls=%async_computation.7 | async-start | bytes 1048576 | tf_op jit(solution)/shard_map/all_to_all | solution.py:278
  120.4 0.0 all-gather.7.cloned.1.call-done
  120.4 9.0 %all-to-all-done.7 = bf16[16,8,2048]{2,1,0:T(8,128)(2,1)S(1)} async-done(((bf16[16,8,2048]{2,1,0:T(8,128)(2,1)}), bf16[16,8,2048]{2,1,0:T(8,128)(2,1)S(1)}, u32[]{:S(2)}, u32[]{:S(2)}) %all-to-all-start.7) | async-done | bytes 524320 | tf_op jit(solution)/shard_map/all_to_all | solution.py:278
  129.4 0.8 copy-done
  130.2 4.5 %mlp.3 = bf16[128,2048]{1,0:T(8,128)(2,1)} custom-call(bf16[128,2048]{1,0:T(8,128)(2,1)} %bitcast.69, bf16[2,8,8,48,256]{4,3,2,1,0:T(8,128)(2,1)} %bitcast.68), custom_call_target="tpu_custom_call" | custom-call | flops 400000000 | bytes 4200000 | tf_op jit(solution)/shard_map/mlp/pallas_call | solution.py:192
  134.7 13.0 %all_to_all.54 = bf16[16,8,2048]{2,1,0:T(8,128)(2,1)S(1)} all-to-all(bf16[16,8,2048]{2,1,0:T(8,128)(2,1)} %bitcast.72), channel_id=1, replica_groups=mesh['section'=2,'tensor'=2,'z'=8,'y'=4,'xh'=2] {'tensor','y','xh'}, dimensions={0} | all-to-all | bytes 1048576 | tf_op jit(solution)/shard_map/all_to_all | solution.py:282
  147.8 0.1 convert_reduce_fusion
  147.8 0.1 fusion.10
  147.9 0.6 pad_maximum_fusion.1
  148.6 6.5 %all-to-all-start.9 = ((bf16[4,8,1024]{2,1,0:T(8,128)(2,1)}), bf16[4,8,1024]{2,1,0:T(8,128)(2,1)S(1)}, u32[]{:S(2)}, u32[]{:S(2)}) async-start(bf16[4,8,1024]{2,1,0:T(8,128)(2,1)} %pad_maximum_fusion.1), calls=%async_computation.9 | async-start | bytes 131072 | tf_op jit(solution)/shard_map/all_to_all | solution.py:297
  155.1 3.3 %all-to-all-done.9 = bf16[4,8,1024]{2,1,0:T(8,128)(2,1)S(1)} async-done(((bf16[4,8,1024]{2,1,0:T(8,128)(2,1)}), bf16[4,8,1024]{2,1,0:T(8,128)(2,1)S(1)}, u32[]{:S(2)}, u32[]{:S(2)}) %all-to-all-start.9) | async-done | bytes 65568 | tf_op jit(solution)/shard_map/all_to_all | solution.py:297
  158.3 0.0 copy-done.1
  158.4 0.7 copy.23
  (23 shorter events, 0.2 us)
Async XLA Ops:
  6.5 19.3 %copy-start.3 = (bf16[8,4,512]{2,1,0:T(4,128)(2,1)S(1)}, bf16[8,4,512]{2,1,0:T(4,128)(2,1)}, u32[]{:S(2)}) copy-start(bf16[8,4,512]{2,1,0:T(4,128)(2,1)} %param.12) | copy-start | bytes 98308
  6.5 25.1 %copy-start.5 = (s32[8]{0:T(128)S(1)}, s32[8]{0:T(128)}, u32[]{:S(2)}) copy-start(s32[8]{0:T(128)} %lens.3) | copy-start | bytes 100
  6.5 63.4 %all-gather.5.cloned.1.call-start = ((), (), s32[]{:S(2)}) async-start(), calls=%async_computation.10 | async-start | bytes 3342336 | tf_op jit(solution)/shard_map/all_gather | solution.py:240
  26.6 8.6 %all-to-all-start = ((bf16[4,32,512]{2,1,0:T(8,128)(2,1)}), bf16[4,32,512]{2,1,0:T(8,128)(2,1)S(1)}, u32[]{:S(2)}, u32[]{:S(2)}) async-start(bf16[4,32,512]{2,1,0:T(8,128)(2,1)} %broadcast_in_dim.27), calls=%async_computation | async-start | bytes 262144 | tf_op jit(solution)/shard_map/all_to_all | solution.py:245
  35.9 19.0 %copy-start.2 = (bf16[4,4,8,512]{3,2,0,1:T(8,128)(2,1)S(1)}, bf16[4,4,8,512]{3,2,0,1:T(8,128)(2,1)}, u32[]{:S(2)}) copy-start(bf16[4,4,8,512]{3,2,0,1:T(8,128)(2,1)} %copy.24) | copy-start | bytes 393220
  35.9 19.1 %copy-start.4 = (f32[1,2048]{1,0:T(1,128)S(1)}, f32[1,2048]{1,0:T(1,128)}, u32[]{:S(2)}) copy-start(f32[1,2048]{1,0:T(1,128)} %param.20) | copy-start | bytes 24580
  46.6 8.2 %all-to-all-start.1 = ((bf16[4,8,2048]{2,1,0:T(8,128)(2,1)}), bf16[4,8,2048]{2,1,0:T(8,128)(2,1)S(1)}, u32[]{:S(2)}, u32[]{:S(2)}) async-start(bf16[4,8,2048]{2,1,0:T(8,128)(2,1)} %attend.2), calls=%async_computation.1 | async-start | bytes 262144 | tf_op jit(solution)/shard_map/all_to_all | solution.py:269
  50.9 69.5 %all-gather.7.cloned.1.call-start = ((), (), s32[]{:S(2)}) async-start(), calls=%async_computation.11 | async-start | bytes 3342336 | tf_op jit(solution)/shard_map/all_gather | solution.py:240
  55.0 1.6 collective-permute-start
  56.7 21.6 %copy-start.6 = (s32[8]{0:T(128)S(1)}, s32[8]{0:T(128)}, u32[]{:S(2)}) copy-start(s32[8]{0:T(128)} %param.13) | copy-start | bytes 100
  74.4 12.5 %all-to-all-start.4 = ((bf16[16,8,2048]{2,1,0:T(8,128)(2,1)}), bf16[16,8,2048]{2,1,0:T(8,128)(2,1)S(1)}, u32[]{:S(2)}, u32[]{:S(2)}) async-start(bf16[16,8,2048]{2,1,0:T(8,128)(2,1)} %bitcast.70), calls=%async_computation.4 | async-start | bytes 1048576 | tf_op jit(solution)/shard_map/all_to_all | solution.py:282
  116.8 12.6 %all-to-all-start.7 = ((bf16[16,8,2048]{2,1,0:T(8,128)(2,1)}), bf16[16,8,2048]{2,1,0:T(8,128)(2,1)S(1)}, u32[]{:S(2)}, u32[]{:S(2)}) async-start(bf16[16,8,2048]{2,1,0:T(8,128)(2,1)} %broadcast_in_dim.55), calls=%async_computation.7 | async-start | bytes 1048576 | tf_op jit(solution)/shard_map/all_to_all | solution.py:278
  120.4 38.0 %copy-start.1 = (bf16[4,8,2048]{2,1,0:T(8,128)(2,1)S(1)}, bf16[4,8,2048]{2,1,0:T(8,128)(2,1)}, u32[]{:S(2)}) copy-start(bf16[4,8,2048]{2,1,0:T(8,128)(2,1)} %all_to_all.52) | copy-start | bytes 393220
  129.4 0.8 copy-start
  148.6 9.8 %all-to-all-start.9 = ((bf16[4,8,1024]{2,1,0:T(8,128)(2,1)}), bf16[4,8,1024]{2,1,0:T(8,128)(2,1)S(1)}, u32[]{:S(2)}, u32[]{:S(2)}) async-start(bf16[4,8,1024]{2,1,0:T(8,128)(2,1)} %pad_maximum_fusion.1), calls=%async_computation.9 | async-start | bytes 131072 | tf_op jit(solution)/shard_map/all_to_all | solution.py:297
Sparse Core Ops, SparseCore 0:
  26.0 41.2 all-gather.4
  69.1 38.9 all-gather.6

commit v2 on v1

v2 whole, which is shorter than its diff:
```python
import functools
import math

import jax
import jax.numpy as jnp
from jax import lax
from jax.experimental import pallas as pl
from jax.experimental.pallas import tpu as pltpu
from jax.sharding import Mesh, PartitionSpec as P

D = 2048
DRAFT = 4
CTX = 384
ROWS = 8
TOKENS = ROWS * DRAFT
HD = 64
QH = 16
KH = 4
SLOTS = CTX * KH
VMEM_LIMIT = 60 * 1024 * 1024
AHEAD = 5
FFS = 256
EPS = 1e-05
THETA = 500000.0
NEGATIVE = -1e30
GROUPS = ((("tensor", "y", "xh"), 16), (("tensor", "y"), 8))
CHIP = ("section", "tensor")
Z = 8


def attend_kernel(
    by_token, lens, me, *refs
):
    pieces, refs = refs[:4], refs[4:]
    gain_h, cos_h, sin_h, wq_h, wkv_h, wo_h, kv_h, *refs = refs
    out, refs = refs[:4], refs[4:]
    kept, half, *refs = refs
    hidden, gain, cosine, sine, wq, wkv, wo, kv, qs, nk, hs, bias, result, sems = refs
    mine = me[0]
    small = []
    small.append(pltpu.make_async_copy(gain_h, gain, sems.at[4]))
    small.append(pltpu.make_async_copy(cos_h, cosine, sems.at[5]))
    small.append(pltpu.make_async_copy(sin_h, sine, sems.at[6]))
    chunks = 8
    step = D // chunks
    copies = []
    for p in range(chunks):
        at = pl.ds(p * step, step)
        copies.append(pltpu.make_async_copy(wq_h.at[at], wq.at[at], sems.at[7 + 2 * p]))
        copies.append(pltpu.make_async_copy(wkv_h.at[at], wkv.at[at], sems.at[8 + 2 * p]))
    base = 7 + 2 * chunks
    kv_copies = [
        pltpu.make_async_copy(kv_h.at[r], kv.at[r], sems.at[base + r]) for r in range(ROWS)
    ]
    wo_copies = [
        pltpu.make_async_copy(
            wo_h.at[pl.ds(p * 256, 256)], wo.at[pl.ds(p * 256, 256)], sems.at[base + ROWS + p]
        )
        for p in range(4)
    ]
    queue = [copies[2 * p : 2 * p + 2] for p in range(chunks)] + [
        kv_copies[2 * p : 2 * p + 2] for p in range(ROWS // 2)
    ]
    queue += [[c] for c in wo_copies]
    for c in small:
        c.start()
    for group in queue[:AHEAD]:
        for c in group:
            c.start()

    def arrived(n):
        for c in queue[n]:
            c.wait()
        if n + AHEAD < len(queue):
            for c in queue[n + AHEAD]:
                c.start()

    row = lax.broadcasted_iota(jnp.int32, (4 * QH, SLOTS), 0)
    place = lax.broadcasted_iota(jnp.int32, (4 * QH, SLOTS), 1)
    bias[...] = jnp.where((place & 3) == (row >> 4), 0.0, NEGATIVE)
    new_row = lax.broadcasted_iota(jnp.int32, (4 * QH, DRAFT * KH), 0)
    new_col = lax.broadcasted_iota(jnp.int32, (4 * QH, DRAFT * KH), 1)
    seen = ((new_col & 3) == (new_row >> 4)) & ((new_col >> 2) <= (new_row & 3))

    for k in range(4):
        other = mine ^ k
        if by_token:
            hidden[other] = pieces[k][...]
        else:
            hidden[:, :, pl.ds(pl.multiple_of(other * 512, 512), 512)] = pieces[k][...]
    for c in small:
        c.wait()
    kept[...] = hidden[mine]
    if by_token:
        half[...] = jnp.where((mine & 1) == 0, hidden[:, :, : D // 2], hidden[:, :, D // 2 :])
    wide = hidden[...].astype(jnp.float32).reshape(TOKENS, D)
    factor = lax.rsqrt(jnp.mean(wide * wide, axis=-1, keepdims=True) + EPS)
    normed = (wide * factor * gain[...]).astype(jnp.bfloat16)
    q = jnp.zeros((TOKENS, QH * HD), jnp.float32)
    new = jnp.zeros((TOKENS, KH * 2 * HD), jnp.float32)
    for p in range(chunks):
        at = pl.ds(p * step, step)
        arrived(p)
        part = normed[:, p * step : (p + 1) * step]
        q = q + jnp.dot(part, wq[at], preferred_element_type=jnp.float32)
        new = new + jnp.dot(part, wkv[at], preferred_element_type=jnp.float32)

    lane = lax.broadcasted_iota(jnp.int32, (TOKENS, 128), 1)
    low = (lane & 63) < 32
    left = lane < HD
    cos_all = cosine[...]
    sin_all = sine[...]

    def turned(block, c, s):
        other = jnp.where(low, pltpu.roll(block, 96, 1), pltpu.roll(block, 32, 1))
        return block * c + other * s

    scale = HD ** (-0.5)
    for m in range(QH // 2):
        block = turned(q[:, m * 128 : (m + 1) * 128], cos_all, sin_all) * scale
        pair = (jnp.where(left, block, 0.0), jnp.where(left, pltpu.roll(block, HD, 1), 0.0))
        for half in range(2):
            for j in range(DRAFT):
                at = ((2 * m + half) * DRAFT + j) * ROWS
                qs[at : at + ROWS, :] = pair[half][j * ROWS : (j + 1) * ROWS, :]
    key_cos = jnp.where(left, cos_all, 1.0)
    key_sin = jnp.where(left, sin_all, 0.0)
    for h in range(KH):
        block = turned(new[:, h * 128 : (h + 1) * 128], key_cos, key_sin)
        for i in range(DRAFT):
            at = (i * KH + h) * ROWS
            nk[at : at + ROWS, :] = block[i * ROWS : (i + 1) * ROWS, :]

    last = (((1,), (1,)), ((), ()))
    for r in range(ROWS):
        fresh = nk[pl.ds(r, DRAFT * KH, stride=ROWS), :].astype(jnp.bfloat16)
        asked = qs[pl.ds(r, 4 * QH, stride=ROWS), :].astype(jnp.bfloat16)
        if r % 2 == 0:
            arrived(chunks + r // 2)
        stored = kv[r]
        scores = lax.dot_general(asked, stored, last, preferred_element_type=jnp.float32)
        scores = jnp.where(place < KH * lens[r], scores, NEGATIVE) + bias[...]
        new_scores = lax.dot_general(asked, fresh, last, preferred_element_type=jnp.float32)
        new_scores = jnp.where(seen, new_scores, NEGATIVE)
        top = jnp.maximum(
            jnp.max(scores, axis=-1, keepdims=True), jnp.max(new_scores, axis=-1, keepdims=True)
        )
        weights = jnp.exp(scores - top)
        new_weights = jnp.exp(new_scores - top)
        total = jnp.sum(weights, axis=-1, keepdims=True) + jnp.sum(
            new_weights, axis=-1, keepdims=True
        )
        mixed = jnp.dot(
            weights.astype(jnp.bfloat16), stored, preferred_element_type=jnp.float32
        ) + jnp.dot(new_weights.astype(jnp.bfloat16), fresh, preferred_element_type=jnp.float32)
        hs[pl.ds(r, 4 * QH, stride=ROWS), :] = mixed / total

    side = lax.broadcasted_iota(jnp.int32, (ROWS, 128), 1) < HD
    rows = []
    for j in range(DRAFT):
        tiles = []
        for m in range(QH // 2):
            first = ((2 * m) * DRAFT + j) * ROWS
            second = ((2 * m + 1) * DRAFT + j) * ROWS
            tiles.append(
                jnp.where(
                    side, pltpu.roll(hs[first : first + ROWS, :], HD, 1), hs[second : second + ROWS, :]
                )
            )
        rows.append(jnp.concatenate(tiles, axis=1))
    heads = jnp.concatenate(rows, axis=0).astype(jnp.bfloat16)
    for p in range(4):
        arrived(chunks + ROWS // 2 + p)
    shares = jnp.dot(heads, wo[...], preferred_element_type=jnp.float32)
    for j in range(DRAFT):
        result[j] = shares[j * ROWS : (j + 1) * ROWS, :].astype(jnp.bfloat16)
    for k in range(4):
        out[k][...] = result[mine ^ k]


def attend(by_token, lens, me, pieces, gain, cosine, sine, wq, wkv, wo, kv):
    hbm = pl.BlockSpec(memory_space=pltpu.HBM)
    vmem = pl.BlockSpec(memory_space=pltpu.VMEM)
    smem = pl.BlockSpec(memory_space=pltpu.SMEM)
    quarter = jax.ShapeDtypeStruct((ROWS, D), jnp.bfloat16)
    return pl.pallas_call(
        functools.partial(attend_kernel, by_token),
        out_shape=[quarter] * 5 + [jax.ShapeDtypeStruct((DRAFT, ROWS, D // 2), jnp.bfloat16)],
        in_specs=[smem] * 2 + [vmem] * 4 + [hbm] * 7,
        out_specs=[vmem] * 6,
        scratch_shapes=[
            pltpu.VMEM((DRAFT, ROWS, D), jnp.bfloat16),
            pltpu.VMEM((1, D), jnp.float32),
            pltpu.VMEM((TOKENS, 128), jnp.float32),
            pltpu.VMEM((TOKENS, 128), jnp.float32),
            pltpu.VMEM((D, QH * HD), jnp.bfloat16),
            pltpu.VMEM((D, KH * 2 * HD), jnp.bfloat16),
            pltpu.VMEM((QH * HD, D), jnp.bfloat16),
            pltpu.VMEM((ROWS, SLOTS, 128), jnp.bfloat16),
            pltpu.VMEM((4 * QH * ROWS, 128), jnp.float32),
            pltpu.VMEM((DRAFT * KH * ROWS, 128), jnp.float32),
            pltpu.VMEM((4 * QH * ROWS, 128), jnp.float32),
            pltpu.VMEM((4 * QH, SLOTS), jnp.float32),
            pltpu.VMEM((DRAFT, ROWS, D), jnp.bfloat16),
            pltpu.SemaphoreType.DMA((35,)),
        ],
        compiler_params=pltpu.CompilerParams(vmem_limit_bytes=VMEM_LIMIT),
        cost_estimate=pl.CostEstimate(flops=400_000_000, transcendentals=800_000, bytes_accessed=13_500_000),
        name="attend",
    )(lens, me, *pieces, gain, cosine, sine, wq, wkv, wo, kv)


def mlp_kernel(tokens_h, gathered, out, tokens, weights, sems):
    token_copy = pltpu.make_async_copy(tokens_h, tokens, sems.at[2 * Z])
    token_copy.start()
    copies = [
        pltpu.make_async_copy(gathered.at[h, z], weights.at[z, :, h], sems.at[2 * z + h])
        for z in range(Z)
        for h in range(2)
    ]
    for c in copies:
        c.start()
    token_copy.wait()
    count = tokens.shape[0]
    units = weights.shape[-1]
    gate = jnp.zeros((count, units), jnp.float32)
    up = jnp.zeros((count, units), jnp.float32)
    for z in range(Z):
        copies[2 * z].wait()
        copies[2 * z + 1].wait()
        part = tokens[:, z * 256 : (z + 1) * 256]
        gate = gate + jnp.dot(
            part, weights[z, :, :, 0:16, :].reshape(256, units), preferred_element_type=jnp.float32
        )
        up = up + jnp.dot(
            part, weights[z, :, :, 16:32, :].reshape(256, units), preferred_element_type=jnp.float32
        )
    act = (gate / (1.0 + jnp.exp(-gate)) * up).astype(jnp.bfloat16)
    for z in range(Z):
        down = weights[z, :, :, 32:48, :].reshape(256, units)
        out[:, z * 256 : (z + 1) * 256] = lax.dot_general(
            act, down, (((1,), (1,)), ((), ())), preferred_element_type=jnp.float32
        ).astype(jnp.bfloat16)


def mlp(tokens, gathered):
    hbm = pl.BlockSpec(memory_space=pltpu.HBM)
    units = gathered.shape[-1]
    return pl.pallas_call(
        mlp_kernel,
        out_shape=jax.ShapeDtypeStruct(tokens.shape, jnp.bfloat16),
        in_specs=[hbm, hbm],
        out_specs=pl.BlockSpec(memory_space=pltpu.VMEM),
        scratch_shapes=[
            pltpu.VMEM(tokens.shape, jnp.bfloat16),
            pltpu.VMEM((Z, 8, 2, 48, units), jnp.bfloat16),
            pltpu.SemaphoreType.DMA((2 * Z + 1,)),
        ],
        compiler_params=pltpu.CompilerParams(vmem_limit_bytes=VMEM_LIMIT),
        cost_estimate=pl.CostEstimate(flops=400_000_000, transcendentals=32768, bytes_accessed=4_200_000),
        name="mlp",
    )(tokens, gathered)


def after(first, then):
    return lax.optimization_barrier((first, then))[1]


def exchanged(blocks):
    return [
        lax.ppermute(blocks[k], CHIP, [(i, i ^ k) for i in range(4)]) for k in (1, 2, 3)
    ]


def normalize(hidden, gain):
    wide = hidden.astype(jnp.float32)
    factor = lax.rsqrt(jnp.mean(wide * wide, axis=-1, keepdims=True) + EPS)
    return (wide * factor * gain).astype(jnp.bfloat16)


def local(
    exit_hidden,
    exit_depth,
    context_len,
    attn_gain,
    w_query,
    w_keyval,
    w_out,
    kv_cache,
    mlp_gain,
    w_gate,
    w_up,
    w_down,
):
    section = lax.axis_index("section")
    tensor = lax.axis_index("tensor")

    def half_rows(which):
        return jnp.stack(
            [lax.dynamic_slice_in_dim(w[0], which * 16, 16, 0) for w in (w_gate, w_up, w_down)]
        )

    own_half = half_rows(section)
    got_half = lax.ppermute(half_rows(1 - section), "section", [(0, 1), (1, 0)])
    first = jnp.where(section == 0, own_half, got_half)
    second = jnp.where(section == 1, own_half, got_half)
    block0 = lax.all_to_all(
        first.reshape(3, 16, 8, FFS).transpose(2, 0, 1, 3).reshape(8, 48, FFS),
        ("y", "xh"),
        0,
        0,
        tiled=True,
    )

    def gathered(block):
        g = lax.all_gather(block, ("section", "z"), axis=0)
        return g.reshape(2, Z, 8, 48, block.shape[-1])

    weights = [gathered(block0)]

    other_gain = lax.ppermute(mlp_gain, "section", [(0, 1), (1, 0)])
    gains = [jnp.where(section == l, mlp_gain, other_gain) for l in range(2)]
    own_piece = after(block0, exit_hidden.transpose(1, 0, 2))
    pieces = [own_piece] + exchanged([own_piece] * 4)
    slices = second.reshape(3, 16, 4, 2 * FFS).transpose(2, 0, 1, 3).reshape(4, 1, 48, 2 * FFS)
    slices = jnp.broadcast_to(slices, (4, 2, 48, 2 * FFS)).reshape(8, 48, 2 * FFS)
    block1 = lax.all_to_all(after(pieces[3], slices), ("y", "xh"), 0, 0, tiled=True)

    where_at = (jnp.arange(DRAFT, dtype=jnp.int32)[:, None] + context_len[None, :]).reshape(TOKENS)
    rates = jnp.exp(jnp.arange(HD // 2, dtype=jnp.float32) * (-2.0 * math.log(THETA) / HD))
    angles = where_at.astype(jnp.float32)[:, None] * rates
    c = jnp.cos(angles)
    s = jnp.sin(angles)
    cosine = jnp.concatenate([c, c, c, c], axis=1)
    sine = jnp.concatenate([-s, s, -s, s], axis=1)

    cache = kv_cache[0].reshape(ROWS, SLOTS, 128)
    me = section * 2 + tensor
    for l in range(2):
        *partial, before, half = attend(
            l == 1,
            context_len,
            me.reshape(1),
            pieces,
            attn_gain,
            cosine,
            sine,
            w_query[0],
            w_keyval[0],
            w_out[0],
            cache,
        )
        near, across, far = exchanged(partial)
        mine = section == l
        mid = (
            before.astype(jnp.float32)
            + jnp.where(mine, partial[0], across).astype(jnp.float32)
            + jnp.where(mine, near, far).astype(jnp.float32)
        ).astype(jnp.bfloat16)
        if l == 0:
            weights.append(gathered(after(mid, block1)))
        mlp_in = normalize(mid, gains[l])
        axes, group = GROUPS[l]
        everyone = lax.all_to_all(
            jnp.broadcast_to(mlp_in[None], (group, ROWS, D)), axes, 0, 0, tiled=True
        )
        share = mlp(everyone.reshape(group * ROWS, D), weights[l])
        shares = lax.all_to_all(share.reshape(group, ROWS, D), axes, 0, 0, tiled=True)
        updated = (mid.astype(jnp.float32) + jnp.sum(shares.astype(jnp.float32), axis=0)).astype(
            jnp.bfloat16
        )
        kept = jnp.where((exit_depth <= l)[:, None], updated, before)
        if l == 0:
            pieces = [kept] + exchanged([kept] * 4)
    left, right = kept[:, : D // 2], kept[:, D // 2 :]
    same = jnp.where(tensor == 0, left, right)
    opposite = jnp.where(tensor == 0, right, left)
    near, across, far = exchanged([same, opposite, same, opposite])
    last = jnp.where(
        tensor == 0, jnp.stack([across, far, same, near]), jnp.stack([far, across, near, same])
    )
    return jnp.where(section == 0, half, last).transpose(1, 0, 2)[None]


def solution(mesh):
    wide = Mesh(mesh.devices.reshape(2, 2, Z, 4, 2), ("section", "tensor", "z", "y", "xh"))
    dp = ("z", "y", "xh")
    in_specs = (
        P(dp, None, ("section", "tensor")),
        P(dp),
        P(dp),
        P("section", None),
        P("section", None, "tensor"),
        P("section", None, "tensor"),
        P("section", "tensor", None),
        P("section", dp, None, "tensor", None),
        P("section", None),
        P("section", dp, "tensor"),
        P("section", dp, "tensor"),
        P("section", dp, "tensor"),
    )
    out_specs = P("section", dp, None, "tensor")
    return jax.shard_map(local, mesh=wide, in_specs=in_specs, out_specs=out_specs, check_vma=False)
```

time: 167 us -> 152 us (0.910)
  blocking collectives: 61.4 us -> 38.1 us
  starting transfers between devices: 24 us -> 33.5 us
  Pallas kernels: 30.4 us -> 28.2 us
    all_to_all x5 -> x3, blocking collectives: 61.4 us -> 38.1 us  [the longest x2 26 us: local(): lax.all_to_all(jnp.broadcast_to(mlp_in[None], (group, ROWS, D)), axes, 0,...]
    ppermute x0 -> x16, starting transfers between devices: none -> 21.4 us  [the longest x15 18.1 us: exchanged(): lax.ppermute(blocks[k], CHIP, [(i, i ^ k) for i in range(4)])]
    all_to_all x5 -> x3, waiting for transfers between devices: 27.5 us -> 14.8 us  [the longest x2 14.8 us: local(): lax.all_to_all(share.reshape(group, ROWS, D), axes, 0, 0, tiled=True)]
    all_to_all x5 -> x3, starting transfers between devices: 23.3 us -> 11.7 us  [the longest x2 8.2 us: local(): lax.all_to_all(share.reshape(group, ROWS, D), axes, 0, 0, tiled=True)]
    ppermute x0 -> x16, waiting for transfers between devices: none -> 11.2 us  [the longest x15 10.1 us: exchanged(): lax.ppermute(blocks[k], CHIP, [(i, i ^ k) for i in range(4)])]
    dynamic_slice x0 -> x2, local copies, waits for them, and re-layouts: none -> 1.84 us  [half_rows(): lax.dynamic_slice_in_dim(w[0], which * 16, 16, 0)]
    unnamed x16 -> x29, local copies, waits for them, and re-layouts: 0.91 us -> 2.73 us
  transfers between devices with their start and end apart: 8 -> 22, of which waited for: 6 -> 10; matrix products, arithmetic and copies ran while one was open for 2% -> 4% of each run, Pallas kernels for 16% -> 16%
where the time goes in v2:
time: 152 us; the launch traced here: 151 us
  blocking collectives  38.1 us (25%)
  starting transfers between devices  33.5 us (22%)
  Pallas kernels  28.2 us (19%)
  waiting for transfers between devices  26.8 us (18%)
  between operations  13.7 us (9%)
  local copies, waits for them, and re-layouts  6.36 us (4%)
  other arithmetic  3.89 us (3%)
    all_to_all x2, blocking collectives, local(): lax.all_to_all(jnp.broadcast_to(mlp_in[None], (group, ROWS, D)), axes, 0,...  26 us
    pallas_call x2, Pallas kernels, attend(): pl.pallas_call(functools.partial(attend_kernel, by_token), out_shape=[qua...  20.1 us
    ppermute x15, starting transfers between devices, exchanged(): lax.ppermute(blocks[k], CHIP, [(i, i ^ k) for i in range(4)])  18.1 us
    all_to_all x2, waiting for transfers between devices, local(): lax.all_to_all(share.reshape(group, ROWS, D), axes, 0, 0, tiled=True)  14.8 us
    all_to_all x1, blocking collectives, local(): lax.all_to_all(first.reshape(3, 16, 8, FFS).transpose(2, 0, 1, 3).reshape...  12.2 us
    ppermute x15, waiting for transfers between devices, exchanged(): lax.ppermute(blocks[k], CHIP, [(i, i ^ k) for i in range(4)])  10.1 us
    all_to_all x2, starting transfers between devices, local(): lax.all_to_all(share.reshape(group, ROWS, D), axes, 0, 0, tiled=True)  8.2 us
    pallas_call x2, Pallas kernels, mlp(): pl.pallas_call(mlp_kernel, out_shape=jax.ShapeDtypeStruct(tokens.shape, j...  8.09 us
  transfers between devices with their start and end apart: 22, of which 10 were waited for; matrix products, arithmetic and copies ran while one was open for 4% of the time, Pallas kernels for 16%

profile of v2, /device:TPU:1, one launch (start us, length us, event | category | flops | bytes accessed | tf_op | source)
XLA Modules:
  0.0 150.6 jit_solution(10135866762116412096)
XLA Ops:
  6.5 0.9 constant_dynamic-slice_fusion.5
  7.4 1.0 constant_dynamic-slice_fusion.3
  8.4 3.3 %collective-permute-start = (bf16[3,16,2048]{2,1,0:T(8,128)(2,1)S(1)}, bf16[3,16,2048]{2,1,0:T(8,128)(2,1)S(1)}, u32[]{:S(2)}, u32[]{:S(2)}) collective-permute-start(bf16[3,16,2048]{2,1,0:T(8,128)(2,1)S(1)} %pad_maximum_fusion.1), channel_id=1, source_target_pairs={{0,128},{128,0},{1,129},{129,1},{2,130},{130,2},{3,131},{131,3},{4... | collective-permute-start | bytes 589832 | tf_op jit(solution)/shard_map/ppermute | solution.py:304
  11.7 1.1 collective-permute-done
  12.8 12.2 %all_to_all.30 = bf16[8,48,256]{2,1,0:T(8,128)(2,1)} all-to-all(bf16[8,48,256]{2,1,0:T(8,128)(2,1)S(1)} %bitcast.49), channel_id=1, replica_groups=mesh['section'=2,'tensor'=2,'z'=8,'y'=4,'xh'=2] {'y','xh'}, dimensions={0} | all-to-all | bytes 393216 | tf_op jit(solution)/shard_map/all_to_all | solution.py:307
  25.0 0.8 copy.25
  25.8 0.7 add_convert_fusion.2
  26.5 0.1 convert_element_type.61
  26.6 2.1 %collective-permute-start.3 = (bf16[4,8,512]{2,1,0:T(8,128)(2,1)S(1)}, bf16[4,8,512]{2,1,0:T(8,128)(2,1)S(1)}, u32[]{:S(2)}, u32[]{:S(2)}) collective-permute-start(bf16[4,8,512]{2,1,0:T(8,128)(2,1)S(1)} %bitcast.52), channel_id=1, source_target_pairs={{0,192},{64,128},{128,64},{192,0},{1,193},{65,129},{129,65},{193,1... | collective-permute-start | bytes 98312 | tf_op jit(solution)/shard_map/ppermute | solution.py:271
  28.7 0.1 fusion.12
  28.8 0.1 reshape.96
  29.0 1.2 collective-permute-start.1
  30.3 0.8 broadcast_in_dim.48
  31.0 3.5 %all-to-all-start.4 = ((bf16[8,48,512]{2,1,0:T(8,128)(2,1)}), bf16[8,48,512]{2,1,0:T(8,128)(2,1)S(1)}, u32[]{:S(2)}, u32[]{:S(2)}) async-start(bf16[8,48,512]{2,1,0:T(8,128)(2,1)} %bitcast.16), calls=%async_computation.4 | async-start | bytes 786432 | tf_op jit(solution)/shard_map/all_to_all | solution.py:327
  34.5 0.7 pad_maximum_fusion.2
  35.3 0.6 copy-done.7
  35.9 10.0 %attend.2 = (bf16[8,2048]{1,0:T(8,128)(2,1)}, bf16[8,2048]{1,0:T(8,128)(2,1)}, bf16[8,2048]{1,0:T(8,128)(2,1)}, bf16[8,2048]{1,0:T(8,128)(2,1)}, bf16[8,2048]{1,0:T(8,128)(2,1)}, /*index=5*/bf16[4,8,1024]{2,1,0:T(8,128)(2,1)}) custom-call(s32[8]{0:T(128)} %lens.3, s32[1]{0:T(128)} %bitcast.me, bf16[4,8,512]{2,1,0:T(8,128)(2,1)} %bitcast.55, ...), custom_call_target="tpu_custom_call" | custom-call | flops 400000000 | bytes 13500000 | tf_op jit(solution)/shard_map/attend/pallas_call | solution.py:186
  45.9 1.8 %collective-permute-start.5 = (bf16[8,2048]{1,0:T(8,128)(2,1)}, bf16[8,2048]{1,0:T(8,128)(2,1)S(1)}, u32[]{:S(2)}, u32[]{:S(2)}) collective-permute-start(bf16[8,2048]{1,0:T(8,128)(2,1)} %get-tuple-element.23), channel_id=1, source_target_pairs={{0,64},{64,0},{128,192},{192,128},{1,65},{65,1},{129,193},{193,129... | collective-permute-start | bytes 98312 | tf_op jit(solution)/shard_map/ppermute | solution.py:271
  47.7 1.4 collective-permute-start.6
  49.1 0.5 collective-permute-done.5
  49.6 2.4 %collective-permute-done.6 = bf16[8,2048]{1,0:T(8,128)(2,1)S(1)} collective-permute-done((bf16[8,2048]{1,0:T(8,128)(2,1)}, bf16[8,2048]{1,0:T(8,128)(2,1)S(1)}, u32[]{:S(2)}, u32[]{:S(2)}) %collective-permute-start.6) | collective-permute-done | bytes 32800 | tf_op jit(solution)/shard_map/ppermute | solution.py:271
  52.0 0.9 fusion
  52.9 0.7 copy-done
  53.7 0.4 collective-permute-start.7
  54.1 0.9 collective-permute-done.7
  55.1 16.7 %all_to_all.31 = bf16[16,8,2048]{2,1,0:T(8,128)(2,1)} all-to-all(bf16[16,8,2048]{2,1,0:T(8,128)(2,1)S(1)} %broadcast_in_dim.24), channel_id=1, replica_groups=mesh['section'=2,'tensor'=2,'z'=8,'y'=4,'xh'=2] {'tensor','y','xh'}, dimensions={0} | all-to-all | bytes 1048576 | tf_op jit(solution)/shard_map/all_to_all | solution.py:364
  71.8 3.5 %mlp.2 = bf16[128,2048]{1,0:T(8,128)(2,1)} custom-call(bf16[128,2048]{1,0:T(8,128)(2,1)} %bitcast.46, bf16[2,8,8,48,256]{4,3,2,1,0:T(8,128)(2,1)} %bitcast.44), custom_call_target="tpu_custom_call" | custom-call | flops 400000000 | bytes 4200000 | tf_op jit(solution)/shard_map/mlp/pallas_call | solution.py:249
  75.3 4.3 %all-to-all-start.2 = ((bf16[16,8,2048]{2,1,0:T(8,128)(2,1)}), bf16[16,8,2048]{2,1,0:T(8,128)(2,1)S(1)}, u32[]{:S(2)}, u32[]{:S(2)}) async-start(bf16[16,8,2048]{2,1,0:T(8,128)(2,1)} %bitcast.45), calls=%async_computation.2 | async-start | bytes 1048576 | tf_op jit(solution)/shard_map/all_to_all | solution.py:368
  79.6 8.7 %all-to-all-done.2 = bf16[16,8,2048]{2,1,0:T(8,128)(2,1)S(1)} async-done(((bf16[16,8,2048]{2,1,0:T(8,128)(2,1)}), bf16[16,8,2048]{2,1,0:T(8,128)(2,1)S(1)}, u32[]{:S(2)}, u32[]{:S(2)}) %all-to-all-start.2) | async-done | bytes 524320 | tf_op jit(solution)/shard_map/all_to_all | solution.py:368
  88.4 0.6 collective-permute-start.8
  89.1 3.3 %collective-permute-start.9 = (bf16[8,2048]{1,0:T(8,128)(2,1)S(1)}, bf16[8,2048]{1,0:T(8,128)(2,1)S(1)}, u32[]{:S(2)}, u32[]{:S(2)}) collective-permute-start(bf16[8,2048]{1,0:T(8,128)(2,1)S(1)} %fusion.11.refs_0_), channel_id=1, source_target_pairs={{0,128},{64,192},{128,0},{192,64},{1,129},{65,193},{129,1},{193,65... | collective-permute-start | bytes 98312 | tf_op jit(solution)/shard_map/ppermute | solution.py:271
  92.4 1.1 collective-permute-start.10
  93.5 2.7 %collective-permute-done.10.refs_3_ = bf16[8,2048]{1,0:T(8,128)(2,1)S(1)} collective-permute-done((bf16[8,2048]{1,0:T(8,128)(2,1)S(1)}, bf16[8,2048]{1,0:T(8,128)(2,1)S(1)}, u32[]{:S(2)}, u32[]{:S(2)}) %collective-permute-start.10) | collective-permute-done | bytes 32800 | tf_op jit(solution)/shard_map/ppermute | solution.py:271
  96.2 0.6 copy-done.11
  96.8 10.1 %attend.3 = (bf16[8,2048]{1,0:T(8,128)(2,1)}, bf16[8,2048]{1,0:T(8,128)(2,1)}, bf16[8,2048]{1,0:T(8,128)(2,1)}, bf16[8,2048]{1,0:T(8,128)(2,1)}, bf16[8,2048]{1,0:T(8,128)(2,1)}, /*index=5*/bf16[4,8,1024]{2,1,0:T(8,128)(2,1)}) custom-call(s32[8]{0:T(128)} %lens.3, s32[1]{0:T(128)} %bitcast.me, bf16[8,2048]{1,0:T(8,128)(2,1)} %copy-done.1, ...), custom_call_target="tpu_custom_call" | custom-call | flops 400000000 | bytes 13500000 | tf_op jit(solution)/shard_map/attend/pallas_call | solution.py:186
  106.8 1.2 collective-permute-start.12
  108.1 1.0 collective-permute-start.13
  109.1 1.2 collective-permute-done.12
  110.3 1.3 collective-permute-done.13
  111.6 0.9 fusion.4
  112.7 9.3 %all_to_all.32 = bf16[8,8,2048]{2,1,0:T(8,128)(2,1)} all-to-all(bf16[8,8,2048]{2,1,0:T(8,128)(2,1)S(1)} %broadcast_in_dim.46), channel_id=1, replica_groups=mesh['section'=2,'tensor'=2,'z'=8,'y'=4,'xh'=2] {'tensor','y'}, dimensions={0} | all-to-all | bytes 524288 | tf_op jit(solution)/shard_map/all_to_all | solution.py:364
  122.0 4.6 %mlp.3 = bf16[64,2048]{1,0:T(8,128)(2,1)} custom-call(bf16[64,2048]{1,0:T(8,128)(2,1)} %bitcast.48, bf16[2,8,8,48,512]{4,3,2,1,0:T(8,128)(2,1)} %bitcast.43), custom_call_target="tpu_custom_call" | custom-call | flops 400000000 | bytes 4200000 | tf_op jit(solution)/shard_map/mlp/pallas_call | solution.py:249
  126.6 3.9 %all-to-all-start.5 = ((bf16[8,8,2048]{2,1,0:T(8,128)(2,1)}), bf16[8,8,2048]{2,1,0:T(8,128)(2,1)S(1)}, u32[]{:S(2)}, u32[]{:S(2)}) async-start(bf16[8,8,2048]{2,1,0:T(8,128)(2,1)} %bitcast.47), calls=%async_computation.5 | async-start | bytes 524288 | tf_op jit(solution)/shard_map/all_to_all | solution.py:368
  130.6 6.1 %all-to-all-done.5 = bf16[8,8,2048]{2,1,0:T(8,128)(2,1)S(1)} async-done(((bf16[8,8,2048]{2,1,0:T(8,128)(2,1)}), bf16[8,8,2048]{2,1,0:T(8,128)(2,1)S(1)}, u32[]{:S(2)}, u32[]{:S(2)}) %all-to-all-start.5) | async-done | bytes 262176 | tf_op jit(solution)/shard_map/all_to_all | solution.py:368
  136.8 0.4 collective-permute-start.16
  137.2 3.8 %collective-permute-start.15 = (bf16[8,1024]{1,0:T(8,128)(2,1)S(1)}, bf16[8,1024]{1,0:T(8,128)(2,1)S(1)}, u32[]{:S(2)}, u32[]{:S(2)}) collective-permute-start(bf16[8,1024]{1,0:T(8,128)(2,1)S(1)} %get-tuple-element.46), channel_id=1, source_target_pairs={{0,192},{64,128},{128,64},{192,0},{1,193},{65,129},{129,65},{193,1... | collective-permute-start | bytes 49160 | tf_op jit(solution)/shard_map/ppermute | solution.py:271
  141.1 1.9 %collective-permute-done.15 = bf16[8,1024]{1,0:T(8,128)(2,1)S(1)} collective-permute-done((bf16[8,1024]{1,0:T(8,128)(2,1)S(1)}, bf16[8,1024]{1,0:T(8,128)(2,1)S(1)}, u32[]{:S(2)}, u32[]{:S(2)}) %collective-permute-start.15) | collective-permute-done | bytes 16416 | tf_op jit(solution)/shard_map/ppermute | solution.py:271
  143.0 0.7 copy.20
  (64 shorter events, 0.9 us)
Async XLA Ops:
  6.5 65.3 %all-gather.5.cloned.1.call-start = ((), (), s32[]{:S(2)}) async-start(), calls=%async_computation.6 | async-start | bytes 3342336 | tf_op jit(solution)/shard_map/all_gather | solution.py:316
  8.4 4.4 %collective-permute-start = (bf16[3,16,2048]{2,1,0:T(8,128)(2,1)S(1)}, bf16[3,16,2048]{2,1,0:T(8,128)(2,1)S(1)}, u32[]{:S(2)}, u32[]{:S(2)}) collective-permute-start(bf16[3,16,2048]{2,1,0:T(8,128)(2,1)S(1)} %pad_maximum_fusion.1), channel_id=1, source_target_pairs={{0,128},{128,0},{1,129},{129,1},{2,130},{130,2},{3,131},{131,3},{4... | collective-permute-start | bytes 589832 | tf_op jit(solution)/shard_map/ppermute | solution.py:304
  25.8 9.5 %copy-start.2 = (bf16[8,4,512]{2,0,1:T(8,128)(2,1)}, bf16[8,4,512]{2,0,1:T(8,128)(2,1)S(1)}, u32[]{:S(2)}) copy-start(bf16[8,4,512]{2,0,1:T(8,128)(2,1)S(1)} %copy.25) | copy-start | bytes 98308
  26.6 3.7 %collective-permute-start.3 = (bf16[4,8,512]{2,1,0:T(8,128)(2,1)S(1)}, bf16[4,8,512]{2,1,0:T(8,128)(2,1)S(1)}, u32[]{:S(2)}, u32[]{:S(2)}) collective-permute-start(bf16[4,8,512]{2,1,0:T(8,128)(2,1)S(1)} %bitcast.52), channel_id=1, source_target_pairs={{0,192},{64,128},{128,64},{192,0},{1,193},{65,129},{129,65},{193,1... | collective-permute-start | bytes 98312 | tf_op jit(solution)/shard_map/ppermute | solution.py:271
  29.0 6.3 %collective-permute-start.1 = (bf16[4,8,512]{2,1,0:T(8,128)(2,1)S(1)}, bf16[4,8,512]{2,1,0:T(8,128)(2,1)S(1)}, u32[]{:S(2)}, u32[]{:S(2)}) collective-permute-start(bf16[4,8,512]{2,1,0:T(8,128)(2,1)S(1)} %bitcast.53), channel_id=1, source_target_pairs={{0,64},{64,0},{128,192},{192,128},{1,65},{65,1},{129,193},{193,129... | collective-permute-start | bytes 98312 | tf_op jit(solution)/shard_map/ppermute | solution.py:271
  30.2 5.0 %collective-permute-start.2 = (bf16[4,8,512]{2,1,0:T(8,128)(2,1)S(1)}, bf16[4,8,512]{2,1,0:T(8,128)(2,1)S(1)}, u32[]{:S(2)}, u32[]{:S(2)}) collective-permute-start(bf16[4,8,512]{2,1,0:T(8,128)(2,1)S(1)} %bitcast.54), channel_id=1, source_target_pairs={{0,128},{64,192},{128,0},{192,64},{1,129},{65,193},{129,1},{193,65... | collective-permute-start | bytes 98312 | tf_op jit(solution)/shard_map/ppermute | solution.py:271
  30.3 5.0 %copy-start.6 = (bf16[4,8,512]{2,1,0:T(8,128)(2,1)}, bf16[4,8,512]{2,1,0:T(8,128)(2,1)S(1)}, u32[]{:S(2)}) copy-start(bf16[4,8,512]{2,1,0:T(8,128)(2,1)S(1)} %collective-permute-done.3.refs_3_) | copy-start | bytes 98308
  31.0 21.9 %all-to-all-start.4 = ((bf16[8,48,512]{2,1,0:T(8,128)(2,1)}), bf16[8,48,512]{2,1,0:T(8,128)(2,1)S(1)}, u32[]{:S(2)}, u32[]{:S(2)}) async-start(bf16[8,48,512]{2,1,0:T(8,128)(2,1)} %bitcast.16), calls=%async_computation.4 | async-start | bytes 786432 | tf_op jit(solution)/shard_map/all_to_all | solution.py:327
  34.5 87.5 %all-gather.7.cloned.1.call-start = ((), (), s32[]{:S(2)}) async-start(), calls=%async_computation.7 | async-start | bytes 6684672 | tf_op jit(solution)/shard_map/all_gather | solution.py:316
  35.2 0.6 copy-start.7
  35.3 0.6 copy-start.8
  35.9 17.8 %copy-start.12 = (f32[1,2048]{1,0:T(1,128)S(1)}, f32[1,2048]{1,0:T(1,128)}, u32[]{:S(2)}) copy-start(f32[1,2048]{1,0:T(1,128)} %param.20) | copy-start | bytes 24580
  45.9 33.7 %copy-start.13 = (s32[8]{0:T(128)S(1)}, s32[8]{0:T(128)}, u32[]{:S(2)}) copy-start(s32[8]{0:T(128)} %param.13) | copy-start | bytes 100
  45.9 42.5 %copy-start.3 = (bf16[8,2048]{1,0:T(8,128)(2,1)S(1)}, bf16[8,2048]{1,0:T(8,128)(2,1)}, u32[]{:S(2)}) copy-start(bf16[8,2048]{1,0:T(8,128)(2,1)} %get-tuple-element.20) | copy-start | bytes 98308
  45.9 3.8 %collective-permute-start.5 = (bf16[8,2048]{1,0:T(8,128)(2,1)}, bf16[8,2048]{1,0:T(8,128)(2,1)S(1)}, u32[]{:S(2)}, u32[]{:S(2)}) collective-permute-start(bf16[8,2048]{1,0:T(8,128)(2,1)} %get-tuple-element.23), channel_id=1, source_target_pairs={{0,64},{64,0},{128,192},{192,128},{1,65},{65,1},{129,193},{193,129... | collective-permute-start | bytes 98312 | tf_op jit(solution)/shard_map/ppermute | solution.py:271
  47.7 4.3 %collective-permute-start.6 = (bf16[8,2048]{1,0:T(8,128)(2,1)}, bf16[8,2048]{1,0:T(8,128)(2,1)S(1)}, u32[]{:S(2)}, u32[]{:S(2)}) collective-permute-start(bf16[8,2048]{1,0:T(8,128)(2,1)} %get-tuple-element.24), channel_id=1, source_target_pairs={{0,192},{64,128},{128,64},{192,0},{1,193},{65,129},{129,65},{193,1... | collective-permute-start | bytes 98312 | tf_op jit(solution)/shard_map/ppermute | solution.py:271
  49.1 2.9 %collective-permute-start.4 = (bf16[8,2048]{1,0:T(8,128)(2,1)}, bf16[8,2048]{1,0:T(8,128)(2,1)S(1)}, u32[]{:S(2)}, u32[]{:S(2)}) collective-permute-start(bf16[8,2048]{1,0:T(8,128)(2,1)} %get-tuple-element.22), channel_id=1, source_target_pairs={{0,128},{64,192},{128,0},{192,64},{1,129},{65,193},{129,1},{193,65... | collective-permute-start | bytes 98312 | tf_op jit(solution)/shard_map/ppermute | solution.py:271
  52.9 0.7 copy-start
  53.7 1.3 collective-permute-start.7
  75.3 12.9 %all-to-all-start.2 = ((bf16[16,8,2048]{2,1,0:T(8,128)(2,1)}), bf16[16,8,2048]{2,1,0:T(8,128)(2,1)S(1)}, u32[]{:S(2)}, u32[]{:S(2)}) async-start(bf16[16,8,2048]{2,1,0:T(8,128)(2,1)} %bitcast.45), calls=%async_computation.2 | async-start | bytes 1048576 | tf_op jit(solution)/shard_map/all_to_all | solution.py:368
  88.4 7.7 %copy-start.1 = (bf16[8,2048]{1,0:T(8,128)(2,1)}, bf16[8,2048]{1,0:T(8,128)(2,1)S(1)}, u32[]{:S(2)}) copy-start(bf16[8,2048]{1,0:T(8,128)(2,1)S(1)} %fusion.11.refs_0_) | copy-start | bytes 98308
  88.4 5.0 %collective-permute-start.8 = (bf16[8,2048]{1,0:T(8,128)(2,1)S(1)}, bf16[8,2048]{1,0:T(8,128)(2,1)S(1)}, u32[]{:S(2)}, u32[]{:S(2)}) collective-permute-start(bf16[8,2048]{1,0:T(8,128)(2,1)S(1)} %fusion.11.refs_0_), channel_id=1, source_target_pairs={{0,64},{64,0},{128,192},{192,128},{1,65},{65,1},{129,193},{193,129... | collective-permute-start | bytes 98312 | tf_op jit(solution)/shard_map/ppermute | solution.py:271
  89.1 4.4 %collective-permute-start.9 = (bf16[8,2048]{1,0:T(8,128)(2,1)S(1)}, bf16[8,2048]{1,0:T(8,128)(2,1)S(1)}, u32[]{:S(2)}, u32[]{:S(2)}) collective-permute-start(bf16[8,2048]{1,0:T(8,128)(2,1)S(1)} %fusion.11.refs_0_), channel_id=1, source_target_pairs={{0,128},{64,192},{128,0},{192,64},{1,129},{65,193},{129,1},{193,65... | collective-permute-start | bytes 98312 | tf_op jit(solution)/shard_map/ppermute | solution.py:271
  92.4 3.8 %collective-permute-start.10 = (bf16[8,2048]{1,0:T(8,128)(2,1)S(1)}, bf16[8,2048]{1,0:T(8,128)(2,1)S(1)}, u32[]{:S(2)}, u32[]{:S(2)}) collective-permute-start(bf16[8,2048]{1,0:T(8,128)(2,1)S(1)} %fusion.11.refs_0_), channel_id=1, source_target_pairs={{0,192},{64,128},{128,64},{192,0},{1,193},{65,129},{129,65},{193,1... | collective-permute-start | bytes 98312 | tf_op jit(solution)/shard_map/ppermute | solution.py:271
  93.5 2.7 %copy-start.9 = (bf16[8,2048]{1,0:T(8,128)(2,1)}, bf16[8,2048]{1,0:T(8,128)(2,1)S(1)}, u32[]{:S(2)}) copy-start(bf16[8,2048]{1,0:T(8,128)(2,1)S(1)} %collective-permute-done.8.refs_1_) | copy-start | bytes 98308
  93.5 2.7 %copy-start.10 = (bf16[8,2048]{1,0:T(8,128)(2,1)}, bf16[8,2048]{1,0:T(8,128)(2,1)S(1)}, u32[]{:S(2)}) copy-start(bf16[8,2048]{1,0:T(8,128)(2,1)S(1)} %collective-permute-done.9.refs_2_) | copy-start | bytes 98308
  96.2 0.6 copy-start.11
  106.8 3.5 %collective-permute-start.12 = (bf16[8,2048]{1,0:T(8,128)(2,1)}, bf16[8,2048]{1,0:T(8,128)(2,1)S(1)}, u32[]{:S(2)}, u32[]{:S(2)}) collective-permute-start(bf16[8,2048]{1,0:T(8,128)(2,1)} %get-tuple-element.29), channel_id=1, source_target_pairs={{0,64},{64,0},{128,192},{192,128},{1,65},{65,1},{129,193},{193,129... | collective-permute-start | bytes 98312 | tf_op jit(solution)/shard_map/ppermute | solution.py:271
  108.1 3.6 %collective-permute-start.13 = (bf16[8,2048]{1,0:T(8,128)(2,1)}, bf16[8,2048]{1,0:T(8,128)(2,1)S(1)}, u32[]{:S(2)}, u32[]{:S(2)}) collective-permute-start(bf16[8,2048]{1,0:T(8,128)(2,1)} %get-tuple-element.30), channel_id=1, source_target_pairs={{0,192},{64,128},{128,64},{192,0},{1,193},{65,129},{129,65},{193,1... | collective-permute-start | bytes 98312 | tf_op jit(solution)/shard_map/ppermute | solution.py:271
  109.1 2.5 %collective-permute-start.11 = (bf16[8,2048]{1,0:T(8,128)(2,1)}, bf16[8,2048]{1,0:T(8,128)(2,1)S(1)}, u32[]{:S(2)}, u32[]{:S(2)}) collective-permute-start(bf16[8,2048]{1,0:T(8,128)(2,1)} %get-tuple-element.28), channel_id=1, source_target_pairs={{0,128},{64,192},{128,0},{192,64},{1,129},{65,193},{129,1},{193,65... | collective-permute-start | bytes 98312 | tf_op jit(solution)/shard_map/ppermute | solution.py:271
  112.7 24.1 %copy-start.4 = (bf16[8,2048]{1,0:T(8,128)(2,1)S(1)}, bf16[8,2048]{1,0:T(8,128)(2,1)}, u32[]{:S(2)}) copy-start(bf16[8,2048]{1,0:T(8,128)(2,1)} %get-tuple-element.26) | copy-start | bytes 98308
  112.7 30.3 %copy-start.5 = (bf16[4,8,1024]{2,1,0:T(8,128)(2,1)S(1)}, bf16[4,8,1024]{2,1,0:T(8,128)(2,1)}, u32[]{:S(2)}) copy-start(bf16[4,8,1024]{2,1,0:T(8,128)(2,1)} %get-tuple-element.25) | copy-start | bytes 196612
  126.6 10.1 %all-to-all-start.5 = ((bf16[8,8,2048]{2,1,0:T(8,128)(2,1)}), bf16[8,8,2048]{2,1,0:T(8,128)(2,1)S(1)}, u32[]{:S(2)}, u32[]{:S(2)}) async-start(bf16[8,8,2048]{2,1,0:T(8,128)(2,1)} %bitcast.47), calls=%async_computation.5 | async-start | bytes 524288 | tf_op jit(solution)/shard_map/all_to_all | solution.py:368
  136.8 4.2 %collective-permute-start.16 = (bf16[8,1024]{1,0:T(8,128)(2,1)S(1)}, bf16[8,1024]{1,0:T(8,128)(2,1)S(1)}, u32[]{:S(2)}, u32[]{:S(2)}) collective-permute-start(bf16[8,1024]{1,0:T(8,128)(2,1)S(1)} %get-tuple-element.46), channel_id=1, source_target_pairs={{0,64},{64,0},{128,192},{192,128},{1,65},{65,1},{129,193},{193,129... | collective-permute-start | bytes 49160 | tf_op jit(solution)/shard_map/ppermute | solution.py:271
  137.2 5.8 %collective-permute-start.15 = (bf16[8,1024]{1,0:T(8,128)(2,1)S(1)}, bf16[8,1024]{1,0:T(8,128)(2,1)S(1)}, u32[]{:S(2)}, u32[]{:S(2)}) collective-permute-start(bf16[8,1024]{1,0:T(8,128)(2,1)S(1)} %get-tuple-element.46), channel_id=1, source_target_pairs={{0,192},{64,128},{128,64},{192,0},{1,193},{65,129},{129,65},{193,1... | collective-permute-start | bytes 49160 | tf_op jit(solution)/shard_map/ppermute | solution.py:271
  141.1 1.9 %collective-permute-start.14 = (bf16[8,1024]{1,0:T(8,128)(2,1)S(1)}, bf16[8,1024]{1,0:T(8,128)(2,1)S(1)}, u32[]{:S(2)}, u32[]{:S(2)}) collective-permute-start(bf16[8,1024]{1,0:T(8,128)(2,1)S(1)} %get-tuple-element.45), channel_id=1, source_target_pairs={{0,128},{64,192},{128,0},{192,64},{1,129},{65,193},{129,1},{193,65... | collective-permute-start | bytes 49160 | tf_op jit(solution)/shard_map/ppermute | solution.py:271
Sparse Core Ops, SparseCore 0:
  25.1 40.9 all-gather.4
  68.0 44.5 all-gather.6
